TPU v7x, 32 devices: a whole 2x2x4 slice. The times are simulated.
32 devices in a mesh: grp: 2 (over core), dp: 4 (over z), mp: 4 (over y, x).
Axes of the slice: x: 2, y: 2, z: 4, core: 2. Of those that a mesh axis runs over, the one named last changes fastest.
Arguments:
- hidden: bfloat16 [1024, 5120], P(('dp', 'mp')), may hold values from -6 to 6
- enc_weight: bfloat16 [5120, 8192], P(None, 'mp'), may hold values from -0.078125 to 0.078125
- enc_bias: bfloat16 [8192], P('mp'), may hold values from -5 to 5
- enc_frozen: bfloat16 [5120, 64], replicated, may hold values from -0.078125 to 0.078125
- enc_adapter: bfloat16 [64, 8192], P(None, 'mp'), may hold values from -0.75 to 0.75
- text_rows: bfloat16 [2560, 8192], P(('dp', 'mp')), may hold values from -6 to 6
- norm_gain: bfloat16 [8192], replicated, may hold values from 0.5 to 1.5
- value_weight: bfloat16 [8192, 1024], P(('dp', 'mp')), may hold values from -0.0625 to 0.0625
- value_bias: bfloat16 [1024], replicated, may hold values from -5 to 5
- llm_frozen: bfloat16 [8192, 64], P(('dp', 'mp')), may hold values from -0.0625 to 0.0625
- llm_adapter: bfloat16 [64, 1024], replicated, may hold values from -0.75 to 0.75
- targets: bfloat16 [2560, 1024], P(('dp', 'mp')), may hold values from -6 to 6
- dest_owner: int32 [1024, 1], replicated, may hold values from 0 to 15; in each aligned block of 256 rows (0 to 255, 256 to 511, ...) at most 32 rows name the same one
- seq_length: int32 [16], P(('dp', 'mp')), may hold values from 128 to 160
Outputs:
- grad_enc: float32 [64, 8192], P('grp', 'mp')
- grad_llm: float32 [64, 1024], P('grp')
Inputs may be any that keep to these rules, and one draw needn't show every extreme that they name: `dest_owner`: within the tokens of one encoder block (aligned blocks of 256 rows) no LLM device is named more than 32 times, and some device is named exactly 32 times in some blocks.
All inputs are finite; a program needn't handle non-finite values.
Results may differ from a plain program's by a relative error of at most 0.003.
Values may be sent and summed in bfloat16 or wider, within the bound.
A program may use at most 128 MiB of HBM per device.

v0:
```python
import jax
import jax.numpy as jnp
from jax import lax
from jax.sharding import PartitionSpec as P

epsilon = 1e-06
F32 = jnp.float32
BF16 = jnp.bfloat16


def swapped(array, axis, bit):
    return lax.ppermute(array, axis, [(i, i ^ 1 << bit) for i in range(lax.axis_size(axis))])


def summed(array, axis):
    for bit in range(lax.axis_size(axis).bit_length() - 1):
        array = array + swapped(array, axis, bit)
    return array


def slot_ranks(destiny, owners):
    markers = (destiny[:, None] == jnp.arange(owners, dtype=jnp.int32)[None, :]).astype(jnp.int32)
    return jnp.sum((jnp.cumsum(markers, axis=0) - markers) * markers, axis=1)


def body(
    hidden,
    enc_weight,
    enc_bias,
    enc_frozen,
    enc_adapter,
    text_rows,
    norm_gain,
    value_weight,
    value_bias,
    llm_frozen,
    llm_adapter,
    targets,
    dest_owner,
    seq_length,
):
    data_ways = lax.axis_size("dp")
    model_ways = lax.axis_size("mp")
    owners = data_ways * model_ways
    core = lax.axis_index("grp")
    lead = core == 0
    block = lax.axis_index("dp")
    member = lax.axis_index("mp")
    owner_index = block * model_ways + member
    own_tokens = hidden.shape[0]
    block_tokens = own_tokens * model_ways
    capacity = 2 * block_tokens // owners
    area = capacity * data_ways
    llm_rows, model_width = text_rows.shape
    rank = enc_frozen.shape[1]
    kv_half = llm_adapter.shape[1] // 2
    col_half = enc_weight.shape[1] // 2

    def half_of(array, axis):
        size = array.shape[axis] // 2
        return lax.dynamic_slice_in_dim(array, core * size, size, axis)

    def in_order(mine, other):
        return jnp.where(lead, mine, other), jnp.where(lead, other, mine)

    part = lax.all_gather(half_of(hidden, 0), "mp", axis=0, tiled=False)
    padding = -(kv_half + rank) % 128
    packed = jnp.concatenate(
        [half_of(value_weight, 1), llm_frozen, jnp.zeros((llm_frozen.shape[0], padding), BF16)],
        axis=1,
    )
    packed, part = lax.optimization_barrier((packed, part))
    weights = lax.all_gather(packed, ("dp", "mp"), axis=0, tiled=True)

    group_rows = jnp.stack(in_order(part, swapped(part, "grp", 0)), axis=1)
    group_rows = group_rows.reshape(block_tokens, hidden.shape[1])
    enc_low = jnp.dot(group_rows, enc_frozen, preferred_element_type=F32).astype(BF16)
    merged = jnp.dot(group_rows, half_of(enc_weight, 1), preferred_element_type=F32)
    merged = merged + half_of(enc_bias, 0).astype(F32)
    merged = merged + jnp.dot(enc_low, half_of(enc_adapter, 1), preferred_element_type=F32)
    merged = merged.astype(BF16).reshape(model_ways, own_tokens, col_half)
    own_cols = lax.all_to_all(merged, "mp", split_axis=0, concat_axis=0, tiled=True)
    first, second = in_order(own_cols, swapped(own_cols, "grp", 0))
    image = jnp.concatenate(
        [piece[k] for k in range(model_ways) for piece in (first, second)], axis=1
    )

    own_targets = half_of(targets, 1)
    head = own_targets[:area].reshape(capacity, data_ways, kv_half)
    head = lax.all_to_all(head, "dp", split_axis=1, concat_axis=1, tiled=True)
    table = lax.all_gather(head, "mp", axis=0, tiled=False)
    table = table.reshape(model_ways * area, kv_half)
    lengths = lax.all_gather(seq_length.astype(F32), ("dp", "mp"), axis=0, tiled=True)
    destiny = dest_owner[:, 0]
    block_dest = lax.dynamic_slice_in_dim(destiny, block * block_tokens, block_tokens)
    block_slot = slot_ranks(block_dest, owners)
    dest = lax.dynamic_slice_in_dim(block_dest, member * own_tokens, own_tokens)
    slot = lax.dynamic_slice_in_dim(block_slot, member * own_tokens, own_tokens)
    index = (dest % model_ways * capacity + slot) * data_ways + dest // model_ways
    picker = (index[:, None] == jnp.arange(model_ways * area, dtype=jnp.int32)[None, :]).astype(BF16)
    image_targets = jnp.dot(picker, table, preferred_element_type=F32)
    owner_marks = dest[:, None] == jnp.arange(owners, dtype=jnp.int32)[None, :]
    image_length = jnp.sum(jnp.where(owner_marks, lengths[None, :], 0.0), axis=1)
    image_place = (slot * data_ways + block).astype(F32)
    image_weight = jnp.where(image_place < image_length, 1.0 / image_length, 0.0)

    counts = jnp.sum(
        (destiny.reshape(data_ways, block_tokens) == owner_index).astype(jnp.int32), axis=1
    )
    position = jnp.arange(llm_rows, dtype=jnp.int32)
    marks = position[:, None] % data_ways == jnp.arange(data_ways, dtype=jnp.int32)[None, :]
    row_count = jnp.sum(jnp.where(marks, counts[None, :], 0), axis=1)
    replaced = (position < area) & (position // data_ways < row_count)
    length = seq_length[0]
    text_weight = jnp.where(
        (position < length) & ~replaced, 1.0 / length.astype(F32), 0.0
    )
    row_weight = jnp.concatenate([image_weight, text_weight])

    gain = norm_gain.astype(F32)

    def norm(rows):
        wide = rows.astype(F32)
        inverse = lax.rsqrt(jnp.mean(wide * wide, axis=1, keepdims=True) + epsilon)
        return (wide * inverse * gain).astype(BF16), inverse

    image_normed, inverse = norm(image)
    text_normed, _ = norm(text_rows)
    normed = jnp.concatenate([image_normed, text_normed], axis=0)
    product = jnp.dot(normed, weights, preferred_element_type=F32)
    low = product[:, kv_half : kv_half + rank].astype(BF16)
    adapter = half_of(llm_adapter, 1)
    values = product[:, :kv_half] + half_of(value_bias, 0).astype(F32)
    values = values + jnp.dot(low, adapter, preferred_element_type=F32)
    all_targets = jnp.concatenate([image_targets, own_targets.astype(F32)], axis=0)
    dvalues = ((values - all_targets) * row_weight[:, None]).astype(BF16)
    grad_llm = jnp.dot(low.T, dvalues, preferred_element_type=F32)

    image_dv = dvalues[:own_tokens]
    dlow = jnp.dot(image_dv, adapter.T, preferred_element_type=F32)
    dlow = (dlow + swapped(dlow, "grp", 0)).astype(BF16)
    dlow = jnp.where(lead, dlow, jnp.zeros_like(dlow))
    sides = jnp.concatenate([image_dv, dlow, jnp.zeros((own_tokens, padding), BF16)], axis=1)
    dnormed = lax.dot_general(
        sides, weights, (((1,), (1,)), ((), ())), preferred_element_type=F32
    )
    pieces = [dnormed[:, k * col_half : (k + 1) * col_half] for k in range(2 * model_ways)]
    even, odd = jnp.stack(pieces[0::2]), jnp.stack(pieces[1::2])
    kept, given = in_order(even, odd)
    dnormed = kept + swapped(given, "grp", 0)
    halves = gain.reshape(model_ways, 2, col_half)
    own_gain = jnp.where(lead, halves[:, 0], halves[:, 1])
    scaled = own_gain[:, None, :] * dnormed
    own_wide = own_cols.astype(F32)
    total = jnp.sum(scaled * own_wide, axis=(0, 2))
    average = ((total + swapped(total, "grp", 0)) / model_width)[None, :, None]
    inv = inverse[None]
    dimage = (inv * scaled - own_wide * (inv * inv * inv) * average).astype(BF16)
    back = lax.all_to_all(dimage, "mp", split_axis=0, concat_axis=0, tiled=True)
    grad_enc = jnp.dot(
        enc_low.T, back.reshape(block_tokens, col_half), preferred_element_type=F32
    )

    grad_llm = summed(grad_llm, "mp")
    grads = summed(jnp.concatenate([grad_enc, grad_llm], axis=1), "dp")
    upper, lower = grads[: rank // 2], grads[rank // 2 :]
    kept, given = in_order(upper, lower)
    first, second = in_order(kept, swapped(given, "grp", 0))
    return (
        jnp.concatenate([first[:, :col_half], second[:, :col_half]], axis=1),
        jnp.concatenate([first[:, col_half:], second[:, col_half:]], axis=1),
    )


def solution(mesh):
    return jax.shard_map(
        body,
        mesh=mesh,
        in_specs=(
            P(("dp", "mp"), None),
            P(None, "mp"),
            P("mp"),
            P(),
            P(None, "mp"),
            P(("dp", "mp"), None),
            P(),
            P(("dp", "mp"), None),
            P(),
            P(("dp", "mp"), None),
            P(),
            P(("dp", "mp"), None),
            P(),
            P(("dp", "mp")),
        ),
        out_specs=(P("grp", "mp"), P("grp", None)),
        check_vma=False,
    )
```

profile of v0, /device:TPU:0, one launch (start us, length us, event | category | flops | bytes accessed | tf_op | source)
XLA Modules:
  0.0 258.4 jit_solution(7647445687864968788)
XLA Ops:
  7.3 1.8 constant_dynamic-slice_fusion.3
  9.2 1.0 copy.25
  10.3 1.0 maximum_maximum_fusion
  11.3 30.0 %all-gather.7.cloned.1.call-done = bf16[128,5120]{1,0:T(8,128)(2,1)} async-done(((bf16[32,5120]{1,0:T(8,128)(2,1)}), bf16[128,5120]{1,0:T(8,128)(2,1)}) %all-gather.7.cloned.1.call-update) | async-done | bytes 1310736 | tf_op jit(solution)/shard_map/all_gather | solution.py:66
  41.4 0.6 reduce-window.6
  43.1 0.7 copy.28
  43.8 0.6 dynamic-slice.3
  44.4 0.7 convert_dynamic-update-slice_fusion
  45.1 42.1 %all-reduce = f32[16]{0:T(128)S(1)} all-reduce(f32[16]{0:T(128)S(1)} %convert_dynamic-update-slice_fusion), channel_id=1, replica_groups=mesh['grp'=2,'dp'=4,'mp'=4] {'dp','mp'}, use_global_device_ids=true, to_apply=%add | all-reduce | flops 16 | bytes 128
  87.6 2.4 fusion.2
  90.1 4.0 %fusion.4 = bf16[160,8192]{1,0:T(8,128)(2,1)} fusion(bf16[160,8192]{1,0:T(8,128)(2,1)} %param.19, f32[8192]{0:T(1024)S(1)} %convert_element_type.74, f32[160]{0:T(256)S(1)} %add_rsqrt_fusion), kind=kLoop, calls=%fused_computation.6 | loop fusion | flops 5242880 | bytes 5276288 | tf_op jit(solution)/shard_map/convert_element_type | solution.py:125
  94.1 0.3 select_bitcast_fusion.1
  94.4 0.2 pad_maximum_fusion
  94.7 0.8 copy-done.4
  95.5 0.9 convolution_convert_fusion
  96.4 5.8 %fusion.12 = f32[256,1024]{1,0:T(8,128)S(1)} fusion(bf16[256,5120]{1,0:T(8,128)(2,1)S(1)} %bitcast.100, bf16[5120,2048]{1,0:T(8,128)(2,1)} %param.15, s32[]{:T(128)S(6)} %select_n.147, f32[1024]{0:T(1024)S(1)} %dynamic-slice_convert_fusion.1), kind=kOutput, calls=%fused_computation.22 | convolution fusion | flops 2684616704 | bytes 14159876 | tf_op jit(solution)/shard_map/dot_general | solution.py:78
  102.2 1.1 fusion.15
  103.4 3.5 %all-to-all-start = ((bf16[4,64,1024]{2,1,0:T(8,128)(2,1)}), bf16[4,64,1024]{2,1,0:T(8,128)(2,1)S(1)}, u32[]{:S(2)}, u32[]{:S(2)}) async-start(bf16[4,64,1024]{2,1,0:T(8,128)(2,1)} %bitcast.5), calls=%async_computation | async-start | bytes 1048576 | tf_op jit(solution)/shard_map/all_to_all | solution.py:82
  106.9 9.0 %all-to-all-done = bf16[4,64,1024]{2,1,0:T(8,128)(2,1)S(1)} async-done(((bf16[4,64,1024]{2,1,0:T(8,128)(2,1)}), bf16[4,64,1024]{2,1,0:T(8,128)(2,1)S(1)}, u32[]{:S(2)}, u32[]{:S(2)}) %all-to-all-start) | async-done | bytes 524320 | tf_op jit(solution)/shard_map/all_to_all | solution.py:82
  115.9 3.3 %all-to-all-start.1 = ((bf16[32,4,512]{2,0,1:T(8,128)(2,1)}), bf16[32,4,512]{2,0,1:T(8,128)(2,1)S(1)}, u32[]{:S(2)}, u32[]{:S(2)}) async-start(bf16[32,4,512]{2,0,1:T(8,128)(2,1)} %copy.28), calls=%async_computation.1 | async-start | bytes 262144 | tf_op jit(solution)/shard_map/all_to_all | solution.py:90
  119.4 9.6 %all-to-all-done.1 = bf16[32,4,512]{2,0,1:T(8,128)(2,1)S(1)} async-done(((bf16[32,4,512]{2,0,1:T(8,128)(2,1)}), bf16[32,4,512]{2,0,1:T(8,128)(2,1)S(1)}, u32[]{:S(2)}, u32[]{:S(2)}) %all-to-all-start.1) | async-done | bytes 131104 | tf_op jit(solution)/shard_map/all_to_all | solution.py:90
  129.1 16.0 %all-gather.1 = bf16[128,4,512]{2,1,0:T(4,128)(2,1)S(1)} all-gather(bf16[32,4,512]{2,1,0:T(4,128)(2,1)S(1)} %copy.29), channel_id=3, replica_groups=mesh['grp'=2,'dp'=4,'mp'=4] {'mp'}, dimensions={0}, use_global_device_ids=true | all-gather | bytes 655360 | tf_op jit(solution)/shard_map/all_gather | solution.py:91
  145.2 0.2 fusion.33
  145.7 0.3 fusion.9
  146.0 0.3 fusion.11
  146.3 33.7 %all-gather.5.cloned.1.call-done = bf16[8192,640]{1,0:T(8,128)(2,1)} async-done(((bf16[512,640]{1,0:T(8,128)(2,1)}), bf16[8192,640]{1,0:T(8,128)(2,1)}) %all-gather.5.cloned.1.call-update) | async-done | bytes 10485776 | tf_op jit(solution)/shard_map/all_gather | solution.py:73
  180.1 7.9 %fusion.5 = f32[224,640]{1,0:T(8,128)S(1)} fusion(bf16[8192,640]{1,0:T(8,128)(2,1)} %all-gather.5.cloned.1.call-done, bf16[160,8192]{1,0:T(8,128)(2,1)} %fusion.4, bf16[64,8192]{1,0:T(8,128)(2,1)S(1)} %fusion.11), kind=kOutput, calls=%fused_computation.7 | convolution fusion | flops 2356150272 | bytes 14729216 | tf_op jit(solution)/shard_map/dot_general | solution.py:130
  188.0 0.2 fusion.18
  188.5 1.2 collective-permute-done.2
  189.7 3.3 %fusion.34 = f32[64,8192]{1,0:T(8,128)S(1)} fusion(bf16[8192,640]{1,0:T(8,128)(2,1)S(1)} %copy-done.2, bf16[64,64]{1,0:T(8,128)(2,1)S(1)} %broadcast.122, bf16[64,64]{1,0:T(8,128)(2,1)S(1)} %fusion.45, bf16[64,512]{1,0:T(8,128)(2,1)S(1)} %slice.134), kind=kOutput, calls=%fused_computation.77 | convolution fusion | flops 671334400 | bytes 12664832 | tf_op jit(solution)/shard_map/dot_general | solution.py:144
  193.0 0.2 slice_bitcast_fusion.7
  193.3 1.1 fusion.23
  194.6 2.8 %collective-permute-done.3 = f32[4,64,1024]{2,1,0:T(8,128)} collective-permute-done((f32[4,64,1024]{2,1,0:T(8,128)}, f32[4,64,1024]{2,1,0:T(8,128)}, u32[]{:S(2)}, u32[]{:S(2)}) %collective-permute-start.3) | collective-permute-done | bytes 1048608 | tf_op jit(solution)/shard_map/ppermute | solution.py:12
  197.4 1.6 fusion.22
  199.0 0.2 collective-permute-start.4
  199.2 1.0 collective-permute-done.4
  200.2 1.1 fusion.21
  201.3 3.5 %all-to-all-start.2 = ((bf16[4,64,1024]{2,1,0:T(8,128)(2,1)}), bf16[4,64,1024]{2,1,0:T(8,128)(2,1)S(1)}, u32[]{:S(2)}, u32[]{:S(2)}) async-start(bf16[4,64,1024]{2,1,0:T(8,128)(2,1)} %fusion.21), calls=%async_computation.2 | async-start | bytes 1048576 | tf_op jit(solution)/shard_map/all_to_all | solution.py:159
  205.0 2.0 collective-permute-start.5
  207.0 9.2 %collective-permute-done.5 = f32[64,512]{1,0:T(8,128)S(1)} collective-permute-done((f32[64,512]{1,0:T(8,128)S(1)}, f32[64,512]{1,0:T(8,128)S(1)}, u32[]{:S(2)}, u32[]{:S(2)}) %collective-permute-start.5) | collective-permute-done | bytes 131104 | tf_op jit(solution)/shard_map/ppermute | solution.py:12
  216.2 1.5 collective-permute-start.6
  217.7 3.5 %collective-permute-done.6 = f32[64,512]{1,0:T(8,128)S(1)} collective-permute-done((f32[64,512]{1,0:T(8,128)S(1)}, f32[64,512]{1,0:T(8,128)S(1)}, u32[]{:S(2)}, u32[]{:S(2)}) %collective-permute-start.6) | collective-permute-done | bytes 131104 | tf_op jit(solution)/shard_map/ppermute | solution.py:12
  221.7 9.1 %collective-permute-done.7 = f32[64,1536]{1,0:T(8,128)S(1)} collective-permute-done((f32[64,1536]{1,0:T(8,128)S(1)}, f32[64,1536]{1,0:T(8,128)S(1)}, u32[]{:S(2)}, u32[]{:S(2)}) %collective-permute-start.7) | collective-permute-done | bytes 393248 | tf_op jit(solution)/shard_map/ppermute | solution.py:12
  230.8 1.7 collective-permute-start.8
  232.5 16.0 %collective-permute-done.8 = f32[64,1536]{1,0:T(8,128)S(1)} collective-permute-done((f32[64,1536]{1,0:T(8,128)S(1)}, f32[64,1536]{1,0:T(8,128)S(1)}, u32[]{:S(2)}, u32[]{:S(2)}) %collective-permute-start.8) | collective-permute-done | bytes 393248 | tf_op jit(solution)/shard_map/ppermute | solution.py:12
  248.7 1.4 collective-permute-done.9
  250.2 0.7 pad_maximum_fusion.5
  250.9 0.7 pad_maximum_fusion.4
  (98 shorter events, 3.3 us)
Async XLA Ops:
  7.2 3.1 %copy-start = (bf16[512,1024]{1,0:T(8,128)(2,1)S(1)}, bf16[512,1024]{1,0:T(8,128)(2,1)}, u32[]{:S(2)}) copy-start(bf16[512,1024]{1,0:T(8,128)(2,1)} %param.21) | copy-start | bytes 3145732
  7.2 36.6 %copy-start.12 = (u32[32]{0:T(128)S(1)}, u32[32]{0:T(128)}, u32[]{:S(2)}) copy-start(u32[32]{0:T(128)} %constant.116) | copy-start | bytes 388
  7.2 34.2 %copy-start.7 = (bf16[8192]{0:T(1024)(128)(2,1)S(1)}, bf16[8192]{0:T(1024)(128)(2,1)}, u32[]{:S(2)}) copy-start(bf16[8192]{0:T(1024)(128)(2,1)} %param.20) | copy-start | bytes 49156
  7.2 34.2 %copy-start.9 = (s32[1024,1]{0,1:T(1,128)S(1)}, s32[1024,1]{0,1:T(1,128)}, u32[]{:S(2)}) copy-start(s32[1024,1]{0,1:T(1,128)} %param.26) | copy-start | bytes 12292
  7.2 35.8 %copy-start.5 = (bf16[160,1024]{1,0:T(8,128)(2,1)S(1)}, bf16[160,1024]{1,0:T(8,128)(2,1)}, u32[]{:S(2)}) copy-start(bf16[160,1024]{1,0:T(8,128)(2,1)} %param.25) | copy-start | bytes 983044
  7.2 34.1 %all-gather.7.cloned.1.call-start = ((), (), s32[]{:S(2)}) async-start(), calls=%async_computation.4 | async-start | bytes 1638400 | tf_op jit(solution)/shard_map/all_gather | solution.py:66
  7.3 80.1 %copy-start.11 = (bf16[1024]{0:T(1024)(128)(2,1)S(1)}, bf16[1024]{0:T(1024)(128)(2,1)}, u32[]{:S(2)}) copy-start(bf16[1024]{0:T(1024)(128)(2,1)} %param.22) | copy-start | bytes 6148
  7.3 80.1 %copy-start.10 = (bf16[2048]{0:T(1024)(128)(2,1)S(1)}, bf16[2048]{0:T(1024)(128)(2,1)}, u32[]{:S(2)}) copy-start(bf16[2048]{0:T(1024)(128)(2,1)} %param.16) | copy-start | bytes 12292
  9.1 170.9 %all-gather.5.cloned.1.call-start = ((), (), s32[]{:S(2)}) async-start(), calls=%async_computation.3 | async-start | bytes 11141120 | tf_op jit(solution)/shard_map/all_gather | solution.py:73
  41.3 48.7 %copy-start.3 = (bf16[128,5120]{1,0:T(8,128)(2,1)S(1)}, bf16[128,5120]{1,0:T(8,128)(2,1)}, u32[]{:S(2)}) copy-start(bf16[128,5120]{1,0:T(8,128)(2,1)} %all-gather.7.cloned.1.call-done) | copy-start | bytes 3932164
  90.0 4.1 %collective-permute-start = (bf16[4,32,5120]{2,1,0:T(8,128)(2,1)S(1)}, bf16[4,32,5120]{2,1,0:T(8,128)(2,1)S(1)}, u32[]{:S(2)}, u32[]{:S(2)}) collective-permute-start(bf16[4,32,5120]{2,1,0:T(8,128)(2,1)S(1)} %bitcast.102), channel_id=1, source_target_pairs={{0,16},{16,0},{1,17},{17,1},{2,18},{18,2},{3,19},{19,3},{4,20},{20... | collective-permute-start | bytes 3932168 | tf_op jit(solution)/shard_map/ppermute | solution.py:12
  94.4 1.1 copy-start.4
  96.4 5.8 %copy-start.6 = (bf16[64,2048]{1,0:T(8,128)(2,1)S(1)}, bf16[64,2048]{1,0:T(8,128)(2,1)}, u32[]{:S(2)}) copy-start(bf16[64,2048]{1,0:T(8,128)(2,1)} %param.18) | copy-start | bytes 786436
  103.4 12.5 %all-to-all-start = ((bf16[4,64,1024]{2,1,0:T(8,128)(2,1)}), bf16[4,64,1024]{2,1,0:T(8,128)(2,1)S(1)}, u32[]{:S(2)}, u32[]{:S(2)}) async-start(bf16[4,64,1024]{2,1,0:T(8,128)(2,1)} %bitcast.5), calls=%async_computation | async-start | bytes 1048576 | tf_op jit(solution)/shard_map/all_to_all | solution.py:82
  115.9 13.1 %all-to-all-start.1 = ((bf16[32,4,512]{2,0,1:T(8,128)(2,1)}), bf16[32,4,512]{2,0,1:T(8,128)(2,1)S(1)}, u32[]{:S(2)}, u32[]{:S(2)}) async-start(bf16[32,4,512]{2,0,1:T(8,128)(2,1)} %copy.28), calls=%async_computation.1 | async-start | bytes 262144 | tf_op jit(solution)/shard_map/all_to_all | solution.py:90
  119.2 26.2 %collective-permute-start.1 = (bf16[4,64,1024]{2,1,0:T(8,128)(2,1)S(1)}, bf16[4,64,1024]{2,1,0:T(8,128)(2,1)S(1)}, u32[]{:S(2)}, u32[]{:S(2)}) collective-permute-start(bf16[4,64,1024]{2,1,0:T(8,128)(2,1)S(1)} %all-to-all-done), channel_id=1, source_target_pairs={{0,16},{16,0},{1,17},{17,1},{2,18},{18,2},{3,19},{19,3},{4,20},{20... | collective-permute-start | bytes 1572872 | tf_op jit(solution)/shard_map/ppermute | solution.py:12
  146.3 41.7 %copy-start.8 = (bf16[64,1024]{1,0:T(8,128)(2,1)S(1)}, bf16[64,1024]{1,0:T(8,128)(2,1)}, u32[]{:S(2)}) copy-start(bf16[64,1024]{1,0:T(8,128)(2,1)} %param.24) | copy-start | bytes 393220
  180.1 9.6 %copy-start.2 = (bf16[8192,640]{1,0:T(8,128)(2,1)S(1)}, bf16[8192,640]{1,0:T(8,128)(2,1)}, u32[]{:S(2)}) copy-start(bf16[8192,640]{1,0:T(8,128)(2,1)} %all-gather.5.cloned.1.call-done) | copy-start | bytes 31457284
  188.4 1.3 collective-permute-start.2
  194.4 3.0 %collective-permute-start.3 = (f32[4,64,1024]{2,1,0:T(8,128)}, f32[4,64,1024]{2,1,0:T(8,128)}, u32[]{:S(2)}, u32[]{:S(2)}) collective-permute-start(f32[4,64,1024]{2,1,0:T(8,128)} %fusion.23), channel_id=1, source_target_pairs={{0,16},{16,0},{1,17},{17,1},{2,18},{18,2},{3,19},{19,3},{4,20},{20... | collective-permute-start | bytes 3145736 | tf_op jit(solution)/shard_map/ppermute | solution.py:12
  199.0 1.2 collective-permute-start.4
  201.3 20.0 %all-to-all-start.2 = ((bf16[4,64,1024]{2,1,0:T(8,128)(2,1)}), bf16[4,64,1024]{2,1,0:T(8,128)(2,1)S(1)}, u32[]{:S(2)}, u32[]{:S(2)}) async-start(bf16[4,64,1024]{2,1,0:T(8,128)(2,1)} %fusion.21), calls=%async_computation.2 | async-start | bytes 1048576 | tf_op jit(solution)/shard_map/all_to_all | solution.py:159
  205.0 11.2 %collective-permute-start.5 = (f32[64,512]{1,0:T(8,128)S(1)}, f32[64,512]{1,0:T(8,128)S(1)}, u32[]{:S(2)}, u32[]{:S(2)}) collective-permute-start(f32[64,512]{1,0:T(8,128)S(1)} %fusion.44), channel_id=1, source_target_pairs={{0,1},{1,0},{2,3},{3,2},{4,5},{5,4},{6,7},{7,6},{8,9},{9,8},{10,11... | collective-permute-start | bytes 393224 | tf_op jit(solution)/shard_map/ppermute | solution.py:12
  216.2 5.0 %collective-permute-start.6 = (f32[64,512]{1,0:T(8,128)S(1)}, f32[64,512]{1,0:T(8,128)S(1)}, u32[]{:S(2)}, u32[]{:S(2)}) collective-permute-start(f32[64,512]{1,0:T(8,128)S(1)} %add.157), channel_id=1, source_target_pairs={{0,2},{1,3},{2,0},{3,1},{4,6},{5,7},{6,4},{7,5},{8,10},{9,11},{10,... | collective-permute-start | bytes 393224 | tf_op jit(solution)/shard_map/ppermute | solution.py:12
  221.5 30.1 %copy-start.1 = (bf16[512,1024]{1,0:T(8,128)(2,1)S(1)}, bf16[512,1024]{1,0:T(8,128)(2,1)}, u32[]{:S(2)}) copy-start(bf16[512,1024]{1,0:T(8,128)(2,1)} %param.21) | copy-start | bytes 3145732
  221.5 9.2 %collective-permute-start.7 = (f32[64,1536]{1,0:T(8,128)S(1)}, f32[64,1536]{1,0:T(8,128)S(1)}, u32[]{:S(2)}, u32[]{:S(2)}) collective-permute-start(f32[64,1536]{1,0:T(8,128)S(1)} %pad_maximum_fusion.3), channel_id=1, source_target_pairs={{0,4},{4,0},{8,12},{12,8},{1,5},{5,1},{9,13},{13,9},{2,6},{6,2},{1... | collective-permute-start | bytes 1179656 | tf_op jit(solution)/shard_map/ppermute | solution.py:12
  230.8 17.7 %collective-permute-start.8 = (f32[64,1536]{1,0:T(8,128)S(1)}, f32[64,1536]{1,0:T(8,128)S(1)}, u32[]{:S(2)}, u32[]{:S(2)}) collective-permute-start(f32[64,1536]{1,0:T(8,128)S(1)} %fusion.63), channel_id=1, source_target_pairs={{0,8},{4,12},{8,0},{12,4},{1,9},{5,13},{9,1},{13,5},{2,10},{6,14},... | collective-permute-start | bytes 1179656 | tf_op jit(solution)/shard_map/ppermute | solution.py:12
  248.6 1.5 collective-permute-start.9
Sparse Core Ops, SparseCore 0:
  9.9 31.3 all-gather.6
  44.0 136.0 all-gather.4
where the time goes:
time: 259 us; the launch traced here: 258 us
  waiting for transfers between devices  126 us (49%)
  blocking collectives  58.1 us (22%)
  matrix products  20.1 us (8%)
  starting transfers between devices  16.5 us (6%)
  other arithmetic  16.1 us (6%)
  between operations  15.3 us (6%)
  local copies, waits for them, and re-layouts  5.9 us (2%)
    ppermute x10, waiting for transfers between devices, swapped(): lax.ppermute(array, axis, [(i, i ^ 1 << bit) for i in range(lax.axis_size...  44.1 us
    unnamed x1, blocking collectives  42.1 us
    all_gather x1, waiting for transfers between devices, body(): weights = lax.all_gather(packed, ('dp', 'mp'), axis=0, tiled=True)  33.7 us
    all_gather x1, waiting for transfers between devices, body(): part = lax.all_gather(half_of(hidden, 0), 'mp', axis=0, tiled=False)  30 us
    all_gather x1, blocking collectives, body(): table = lax.all_gather(head, 'mp', axis=0, tiled=False)  16 us
    all_to_all x1, waiting for transfers between devices, body(): head = lax.all_to_all(head, 'dp', split_axis=1, concat_axis=1, tiled=True)  9.57 us
    all_to_all x1, waiting for transfers between devices, body(): lax.all_to_all(merged, 'mp', split_axis=0, concat_axis=0, tiled=True)  8.97 us
    dot_general x1, matrix products, body(): product = jnp.dot(normed, weights, preferred_element_type=F32)  7.93 us
  transfers between devices with their start and end apart: 15, of which 12 were waited for; matrix products, arithmetic and copies ran while one was open for 9% of the time, Pallas kernels for 0%

commit v1 on v0

v1 whole, which is shorter than its diff:
```python
import functools

import jax
import jax.numpy as jnp
from jax import lax
from jax.experimental import pallas as pl
from jax.experimental.pallas import tpu as pltpu
from jax.sharding import PartitionSpec as P

epsilon = 1e-06
F32 = jnp.float32
BF16 = jnp.bfloat16
MESH = pl.DeviceIdType.MESH
NN = (((1,), (0,)), ((), ()))
NT = (((1,), (1,)), ((), ()))


def dot(a, b, dims=NN):
    return lax.dot_general(a, b, dims, preferred_element_type=F32)


def split(x):
    high = x.astype(BF16)
    rest = (x - high.astype(F32)).astype(BF16)
    return jnp.concatenate([high, rest], axis=0)


def joined(x):
    half = x.shape[0] // 2
    return x[:half] + x[half:]


def eye(n):
    return (
        lax.broadcasted_iota(jnp.int32, (n, n), 0) == lax.broadcasted_iota(jnp.int32, (n, n), 1)
    ).astype(BF16)


def kernel(
    sizes,
    hidden, enc_weight, enc_bias, enc_frozen, enc_adapter, text_rows, gain_ref, value_weight,
    bias_ref, llm_frozen, adapter_ref, targets, dest, seq_length,
    out_enc, out_llm,
    ebuf, hid, acc, acc_low, img, xq, xr, wq, at, txt, gs, gr, tgs, tgr, los, lor,
    vown, vps, vpr, vs, vr, ys, yr, yrs, yrr, ss, sr, hys, hyr, hbs, hb, yos, s2s, s2r, fo,
    e_sem, t_sem, own_sem, h_ss, h_rs, hf_ss, hf_rs, w_ss, w_rs, a1_ss, a1_rs, a2_ss, a2_rs,
    a3_ss, a3_rs, tg_ss, tg_rs, x_ss, x_rs, lo_ss, lo_rs, g_ss, g_rs, vp_ss, vp_rs, v_ss, v_rs,
    yp_ss, yp_rs, yr_ss, yr_rs, s_ss, s_rs, hy_ss, hy_rs, hb_ss, hb_rs, yo_ss, yo_rs,
    s2_ss, s2_rs, fo_ss, fo_rs,
):
    z = sizes
    DP, MP = z["DP"], z["MP"]
    NTOK, BT, CAP, ST, LR = z["NTOK"], z["BT"], z["CAP"], z["ST"], z["LR"]
    D, MH, RANK, KV, NB = z["D"], z["MH"], z["RANK"], z["KV"], z["NB"]
    SH, HC, Q, R, UN, RU, RD, RG, KC = (z[k] for k in ("SH", "HC", "Q", "R", "UN", "RU", "RD", "RG", "KC"))
    KH = KV // 2
    NK = MH // KC
    QB = Q // R
    OWN = DP * MP
    c = lax.axis_index("grp")
    e = lax.axis_index("dp")
    m = lax.axis_index("mp")
    p, u = e % 2, e // 2
    oc = 1 - c
    t0 = (p + m // 2 + c) % 2
    owner = e * MP + m
    pending = []

    def copy(src, dst, ssem, rsem, dp=None, mp=None, grp=None):
        device = {"grp": c if grp is None else grp, "dp": e if dp is None else dp, "mp": m if mp is None else mp}
        return pltpu.make_async_remote_copy(
            src_ref=src, dst_ref=dst, send_sem=ssem, recv_sem=rsem, device_id=device, device_id_type=MESH
        )

    def send(*args, **kw):
        made = copy(*args, **kw)
        made.start()
        pending.append(made)

    def landed(dst, ssem, rsem):
        copy(dst, dst, ssem, rsem, grp=oc).wait_recv()

    half = c * HC
    loads = []
    for k in range(NK):
        one = pltpu.make_async_copy(
            enc_weight.at[pl.ds(k * KC, KC), pl.ds(half, HC)], ebuf.at[pl.ds(k * KC, KC), :], e_sem.at[k]
        )
        loads.append(one)
    text_load = pltpu.make_async_copy(text_rows, txt, t_sem)
    own_load = pltpu.make_async_copy(hidden, hid.at[pl.ds(m * NTOK, NTOK), :], own_sem)
    own_load.start()
    text_load.start()
    for one in loads:
        one.start()

    RH = RANK // 2
    low_half = c * RH
    at_own = dot(eye(RANK), llm_frozen[...], NT).astype(BF16)
    at[e, m, pl.ds(low_half, RH), :] = jnp.where(c == 0, at_own[:RH], at_own[RH:])
    rows = CAP * DP
    order_i = lax.broadcasted_iota(jnp.int32, (rows, rows), 0)
    order_j = lax.broadcasted_iota(jnp.int32, (rows, rows), 1)
    order = (order_j == order_i % CAP * DP + order_i // CAP).astype(BF16)
    sorted_targets = dot(order, targets[pl.ds(0, rows), pl.ds(c * KH, KH)]).astype(BF16)
    length = seq_length[...].astype(F32)
    for i in range(DP):
        for j in range(MP):
            block = sorted_targets[i * CAP : (i + 1) * CAP, j * NB : (j + 1) * NB]
            tail = jnp.broadcast_to(length, (ST - CAP, NB)).astype(BF16)
            tgs[i, j] = jnp.concatenate([block, tail], axis=0)

    barrier = pltpu.get_barrier_semaphore()
    devices = 2 * OWN
    place = (c * DP + e) * MP + m

    def greet(i, carry):
        other = (place + i) % devices
        device = {"grp": other // OWN, "dp": other // MP % DP, "mp": other % MP}
        pl.semaphore_signal(barrier, inc=1, device_id=device, device_id_type=MESH)
        return carry

    lax.fori_loop(1, devices, greet, 0)
    pl.semaphore_wait(barrier, devices - 1)

    for i in range(1, DP):
        mine = at.at[e, m, pl.ds(low_half, RH), :]
        send(mine, mine, a1_ss.at[i], a1_rs.at[i], dp=(e + i) % DP)
    NH = NTOK // 2
    hid_rows = pl.ds(m * NTOK + c * NH, NH)
    for k in range(NK):
        cols = pl.ds(k * KC, KC)
        for i in range(1, MP):
            send(hidden.at[pl.ds(c * NH, NH), cols], hid.at[hid_rows, cols], h_ss.at[k, i], h_rs.at[k, i], mp=(m + i) % MP)
    w_row = owner * R
    w_m = w_row // SH
    w_t = w_row % SH // Q
    w_slot = w_row % Q // R
    w_core = w_t // 2
    w_par = (w_t % 2 + w_t // 2 + w_m // 2) % 2
    w_sends = []
    for i in range((UN + 1) // 2):
        w_u = 2 * i + c
        there = 2 * w_u + w_par
        self_case = (there == e) & (w_m == m) & (w_core == c)
        live = w_u < UN
        away = copy(value_weight, wq.at[w_slot], w_ss.at[i], w_rs.at[w_slot], dp=there, mp=w_m, grp=w_core)
        near = pltpu.make_async_copy(value_weight, wq.at[w_slot], w_rs.at[w_slot])
        w_sends.append((live & jnp.logical_not(self_case), away))

        @pl.when(live & jnp.logical_not(self_case))
        def _():
            away.start()

        @pl.when(live & self_case)
        def _():
            near.start()

    for i in range(1, OWN):
        other = (owner + i) % OWN
        od, om = other // MP, other % MP
        send(tgs.at[od, om], tgr.at[e, m], tg_ss.at[i], tg_rs.at[i], dp=od, mp=om)
    tgr[e, m] = tgs[e, m]

    text_load.wait()
    TR = 16
    CW = min(D, 1024)

    def text_norm(i, carry):
        r = pl.ds(i * TR, TR)
        total = jnp.zeros((TR, 128), F32)
        for k in range(D // CW):
            part = txt[r, pl.ds(k * CW, CW)].astype(F32)
            part = part * part
            for n in range(CW // 128):
                total = total + part[:, n * 128 : (n + 1) * 128]
        inverse = lax.rsqrt(jnp.sum(total, axis=1, keepdims=True) / D + epsilon)
        for k in range(D // CW):
            cols = pl.ds(k * CW, CW)
            txt[r, cols] = (txt[r, cols].astype(F32) * inverse * gain_ref[:, cols].astype(F32)).astype(BF16)
        return carry

    lax.fori_loop(0, LR // TR, text_norm, 0)

    for i in range(1, DP):
        there = at.at[(e + DP - i) % DP, m, pl.ds(low_half, RH), :]
        landed(there, a1_ss.at[i], a1_rs.at[i])
    for i in range(1, MP):
        mine = at.at[:, m, pl.ds(low_half, RH), :]
        send(mine, mine, a2_ss.at[i], a2_rs.at[i], mp=(m + i) % MP)

    own_load.wait()
    TN = min(HC, 256)
    for k in range(NK):
        cols = pl.ds(k * KC, KC)
        for i in range(1, MP):
            peer = (m + MP - i) % MP
            there = hid.at[pl.ds(peer * NTOK + c * NH, NH), cols]
            landed(there, h_ss.at[k, i], h_rs.at[k, i])
            send(there, there, hf_ss.at[k, i], hf_rs.at[k, i], grp=oc)
        loads[k].wait()
        for i in range(1, MP):
            peer = (m + MP - i) % MP
            there = hid.at[pl.ds(peer * NTOK + oc * NH, NH), cols]
            landed(there, hf_ss.at[k, i], hf_rs.at[k, i])

        def product(n, carry):
            part = dot(hid[:, cols], ebuf[cols, pl.ds(n * TN, TN)])
            if k == 0:
                acc[:, pl.ds(n * TN, TN)] = part
            else:
                acc[:, pl.ds(n * TN, TN)] += part
            return carry

        lax.fori_loop(0, HC // TN, product, 0)
        low_part = dot(hid[:, cols], enc_frozen[cols, :])
        if k == 0:
            acc_low[...] = low_part
        else:
            acc_low[...] += low_part
    enc_low = acc_low[...].astype(BF16)
    enc_low_t = dot(eye(RANK), enc_low, NT)
    squares = jnp.zeros((BT, 128), F32)
    for n in range(HC // TN):
        cols = pl.ds(n * TN, TN)
        shifted = pl.ds(half + n * TN, TN)
        merged = acc[:, cols] + enc_bias[:, shifted].astype(F32) + dot(enc_low, enc_adapter[:, shifted])
        merged = merged.astype(BF16)
        img[:, cols] = merged
        wide = merged.astype(F32)
        square = wide * wide
        for i in range(TN // 128):
            squares = squares + square[:, i * 128 : (i + 1) * 128]
        scaled = (wide * gain_ref[:, pl.ds(m * SH + half + n * TN, TN)].astype(F32)).astype(BF16)
        xq[n * TN // Q, :, n * TN % Q : n * TN % Q + TN] = scaled
    pair = e + 1 - 2 * p
    send(xq.at[1 - t0], xr, x_ss, x_rs, dp=pair)

    for i in range(1, MP):
        there = at.at[:, (m + MP - i) % MP, pl.ds(low_half, RH), :]
        landed(there, a2_ss.at[i], a2_rs.at[i])
    mine = at.at[:, :, pl.ds(low_half, RH), :]
    send(mine, mine, a3_ss, a3_rs, grp=oc)
    landed(at.at[:, :, pl.ds(oc * RH, RH), :], a3_ss, a3_rs)

    first = (m * SH + half) // R
    low_part = jnp.zeros((RANK, BT), F32)
    for i in range(HC // R):
        q = first + i
        x = xq[i * R // Q, :, i * R % Q : i * R % Q + R]
        low_part = low_part + dot(at[q // MP, q % MP], x, NT)
    total = jnp.broadcast_to(jnp.sum(squares, axis=1, keepdims=True), (BT, 128))
    los[...] = jnp.concatenate([low_part, total.T[:8]], axis=0)
    me8 = m * 2 + c
    for i in range(1, 2 * MP):
        other = (me8 + i) % (2 * MP)
        send(los, lor.at[me8], lo_ss.at[i], lo_rs.at[i], mp=other // 2, grp=other % 2)
    lor[me8] = los[...]

    def text_low(q, carry):
        lt, ln = carry
        part = txt[:, pl.ds(pl.multiple_of(q * R, 128), R)]
        a = at[q // MP, q % MP]
        return lt + dot(a, part, NT), ln + dot(part, a, NT)

    text_low_t, text_low_n = lax.fori_loop(
        0, OWN, text_low, (jnp.zeros((RANK, LR), F32), jnp.zeros((LR, RANK), F32))
    )
    place_row = lax.broadcasted_iota(jnp.int32, (8, LR), 1)
    count = jnp.zeros((8, LR), F32)
    for i in range(DP):
        named = (dest[pl.ds(i * BT, BT), :] == owner).astype(F32)
        named = jnp.sum(named, axis=0, keepdims=True)
        count = jnp.where(place_row % DP == i, jnp.broadcast_to(named, (8, LR)), count)
    replaced = (place_row < CAP * DP) & ((place_row // DP).astype(F32) < count)
    live = (place_row.astype(F32) < jnp.broadcast_to(length, (8, LR))) & jnp.logical_not(replaced)
    live = jnp.where(live, 1.0, 0.0)[:1]
    text_low_m = (text_low_t.astype(BF16).astype(F32) * live).astype(BF16)
    text_low_b = text_low_n.astype(BF16)
    scale = 1.0 / length
    here8 = p * MP + m
    for j in range(MP):
        for i in range(2):
            col = pl.multiple_of(j * SH + half + i * Q, 128)
            gs[j, i] = (dot(text_low_m, txt[:, pl.ds(col, Q)]) * scale).astype(BF16)
    for i in range(1, 2 * MP):
        other = (here8 + i) % (2 * MP)
        gp, gm = other // MP, other % MP
        send(gs.at[gm, (gp + gm // 2 + c) % 2], gr.at[p, m], g_ss.at[i], g_rs.at[i], dp=2 * u + gp, mp=gm)
    gr[p, m] = gs[m, t0]
    text_y = dot(text_low_b, adapter_ref[:, pl.ds(c * KH, KH)])
    text_y = text_y + bias_ref[:, pl.ds(c * KH, KH)].astype(F32) - targets[:, pl.ds(c * KH, KH)].astype(F32)
    high = text_y.astype(BF16)
    rest = (text_y - high.astype(F32)).astype(BF16)
    text_grad = (dot(text_low_m, high) + dot(text_low_m, rest)) * scale

    for i in range(1, OWN):
        other = (owner + OWN - i) % OWN
        landed(tgr.at[other // MP, other % MP], tg_ss.at[i], tg_rs.at[i])
    block_dest = dest[pl.ds(pl.multiple_of(e * BT, 8), BT), :]
    marks = block_dest == lax.broadcasted_iota(jnp.int32, (BT, 128), 1)
    before = lax.broadcasted_iota(jnp.int32, (BT, BT), 0) > lax.broadcasted_iota(jnp.int32, (BT, BT), 1)
    counted = dot(before.astype(BF16), marks.astype(BF16))
    slot = jnp.sum(jnp.where(marks, counted, 0.0), axis=1, keepdims=True)
    base = block_dest.astype(F32) * ST
    table_rows = lax.broadcasted_iota(jnp.int32, (BT, OWN * ST), 1).astype(F32)
    table = tgr[...].reshape(OWN * ST, NB)
    image_targets = dot((table_rows == base + slot).astype(BF16), table)
    image_length = dot((table_rows == base + CAP).astype(BF16), table)
    position = slot * DP + e.astype(F32)
    weight = jnp.where(position < image_length, 1.0 / image_length, 0.0)

    gathered = jnp.zeros((RANK + 8, BT), F32)
    for i in range(1, 2 * MP):
        other = (me8 + 2 * MP - i) % (2 * MP)
        landed(lor.at[other], lo_ss.at[i], lo_rs.at[i])
    for i in range(2 * MP):
        gathered = gathered + lor[i]
    inverse_row = lax.rsqrt(gathered[RANK : RANK + 1] / D + epsilon)
    low_t = (gathered[:RANK] * inverse_row).astype(BF16)
    turned = jnp.concatenate(
        [low_t.astype(F32), jnp.broadcast_to(inverse_row, (128 - RANK, BT))], axis=0
    ).T
    low = turned[:, :RANK].astype(BF16)
    inverse = turned[:, RANK : RANK + 1]

    for i in range(QB):
        landed(wq.at[i], w_ss.at[0], w_rs.at[i])

    def values_of(x, where, first_col):
        for n in range(KH // TN):
            cols = pl.ds(pl.multiple_of(first_col + n * TN, 128), TN)
            part = dot(x[:, :R], wq[0, :, cols])
            for i in range(1, QB):
                part = part + dot(x[:, i * R : (i + 1) * R], wq[i, :, cols])
            where[:, n * TN : (n + 1) * TN] = part.astype(where.dtype)

    values_of(xq[t0], vps.at[p], oc * KH)
    send(vps.at[p], vpr.at[p], vp_ss.at[0], vp_rs.at[0], grp=oc)
    landed(xr, x_ss, x_rs)
    values_of(xr[...], vps.at[1 - p], oc * KH)
    send(vps.at[1 - p], vpr.at[1 - p], vp_ss.at[1], vp_rs.at[1], grp=oc)
    values_of(xq[t0], vown.at[p], c * KH)
    values_of(xr[...], vown.at[1 - p], c * KH)
    landed(vpr.at[p], vp_ss.at[0], vp_rs.at[0])
    landed(vpr.at[1 - p], vp_ss.at[1], vp_rs.at[1])
    for i in range(2):
        both = (vown[i] + vpr[i].astype(F32)).astype(BF16)
        for j in range(MP):
            vs[i, j] = both[:, j * NB : (j + 1) * NB]
    for i in range(1, 2 * MP):
        other = (here8 + i) % (2 * MP)
        gp, gm = other // MP, other % MP
        send(vs.at[gp, gm], vr.at[p, m], v_ss.at[i], v_rs.at[i], dp=2 * u + gp, mp=gm)
    vr[p, m] = vs[p, m]

    for i in range(1, 2 * MP):
        other = (here8 + 2 * MP - i) % (2 * MP)
        landed(gr.at[other // MP, other % MP], g_ss.at[i], g_rs.at[i])
    g_sum = jnp.zeros((RANK, Q), F32)
    for i in range(2):
        for j in range(MP):
            g_sum = g_sum + gr[i, j].astype(F32)
    g_pair = split(g_sum)

    def through(cols):
        part = dot(g_pair[:, :R], wq[0, :, cols])
        for i in range(1, QB):
            part = part + dot(g_pair[:, i * R : (i + 1) * R], wq[i, :, cols])
        return joined(part)

    ys[...] = through(pl.ds(oc * KH, KH))
    send(ys, yr, yp_ss, yp_rs, grp=oc)
    text_grad = text_grad + through(pl.ds(c * KH, KH))
    landed(yr, yp_ss, yp_rs)
    text_grad = text_grad + yr[...]
    for i in range(DP):
        for j in range(MP):
            yrs[i, j] = text_grad[i * RD : (i + 1) * RD, j * NB : (j + 1) * NB]
    for i in range(1, OWN):
        other = (owner + i) % OWN
        od, om = other // MP, other % MP
        send(yrs.at[od, om], yrr.at[e, m], yr_ss.at[i], yr_rs.at[i], dp=od, mp=om)
    yrr[e, m] = yrs[e, m]

    for i in range(1, 2 * MP):
        other = (here8 + 2 * MP - i) % (2 * MP)
        landed(vr.at[other // MP, other % MP], v_ss.at[i], v_rs.at[i])
    product_sum = jnp.zeros((BT, NB), F32)
    for i in range(2):
        for j in range(MP):
            product_sum = product_sum + vr[i, j].astype(F32)
    own_cols = pl.ds(pl.multiple_of(c * KH + m * NB, 128), NB)
    plain = product_sum * inverse + dot(low, adapter_ref[:, own_cols])
    dv = plain + bias_ref[:, own_cols].astype(F32) - image_targets
    dv = (dv * weight).astype(BF16)
    along = jnp.sum(dv.astype(F32) * plain, axis=1, keepdims=True)
    ss[...] = jnp.broadcast_to(along, (BT, 128)).T[:8]
    for i in range(1, 2 * MP):
        other = (me8 + i) % (2 * MP)
        send(ss, sr.at[me8], s_ss.at[i], s_rs.at[i], mp=other // 2, grp=other % 2)
    sr[me8] = ss[...]
    h_part = joined(dot(split(enc_low_t * inverse_row), dv))
    y_part = dot(low_t, dv)
    for i in range(DP):
        hys[i, 0] = h_part[i * RD : (i + 1) * RD]
        hys[i, 1] = y_part[i * RD : (i + 1) * RD]
    for i in range(1, DP):
        there = (e + i) % DP
        send(hys.at[there], hyr.at[e], hy_ss.at[i], hy_rs.at[i], dp=there)
    hyr[e] = hys[e]

    for i in range(1, 2 * MP):
        other = (me8 + 2 * MP - i) % (2 * MP)
        landed(sr.at[other], s_ss.at[i], s_rs.at[i])
    along_row = jnp.zeros((8, BT), F32)
    for i in range(2 * MP):
        along_row = along_row + sr[i]
    factor = along_row[:1] * inverse_row * inverse_row / D
    second_pair = split(enc_low_t * factor)
    for i in range(2):
        second = joined(dot(second_pair, img[:, pl.ds(i * Q, Q)])).astype(BF16)
        for j in range(UN):
            s2s[i, j] = second[j * RU : (j + 1) * RU]
    for i in range(1, DP):
        there = (e + i) % DP
        send(s2s.at[(there % 2 + c + m // 2) % 2, there // 2], s2r.at[e], s2_ss.at[i], s2_rs.at[i], dp=there)
    s2r[e] = s2s[t0, u]

    for i in range(1, DP):
        landed(hyr.at[(e + DP - i) % DP], hy_ss.at[i], hy_rs.at[i])
    hy = hyr[0]
    for i in range(1, DP):
        hy = hy + hyr[i]
    hbs[...] = hy[0]
    unit = (p * 2 + c) * MP + m
    for i in range(1, 4 * MP):
        other = (unit + i) % (4 * MP)
        send(
            hbs, hb.at[p, c, m], hb_ss.at[i], hb_rs.at[i],
            dp=2 * u + other // (2 * MP), grp=other // MP % 2, mp=other % MP,
        )
    hb[p, c, m] = hbs[...]
    for i in range(1, OWN):
        other = (owner + OWN - i) % OWN
        landed(yrr.at[other // MP, other % MP], yr_ss.at[i], yr_rs.at[i])
    y_sum = hy[1]
    for i in range(DP):
        for j in range(MP):
            y_sum = y_sum + yrr[i, j]
    yos[...] = y_sum
    DH = DP // 2
    y_core = e // DH
    y_row = e % DH
    y_there = out_llm.at[y_row, :, own_cols]
    for i in range(1, OWN):
        other = (owner + i) % OWN
        send(yos, y_there, yo_ss.at[i], yo_rs.at[y_row, m, c], dp=other // MP, mp=other % MP, grp=y_core)
    y_away = copy(yos, y_there, yo_ss.at[0], yo_rs.at[y_row, m, c], grp=oc)

    @pl.when(y_core == c)
    def _():
        out_llm[y_row, :, own_cols] = yos[...]

    @pl.when(y_core != c)
    def _():
        y_away.start()

    for i in range(1, 4 * MP):
        other = (unit + 4 * MP - i) % (4 * MP)
        landed(hb.at[other // (2 * MP), other // MP % 2, other % MP], hb_ss.at[i], hb_rs.at[i])
    h_all = jnp.concatenate(
        [
            jnp.concatenate([hb[i, j, k] for j in range(2) for k in range(MP)], axis=1)
            for i in range(2)
        ],
        axis=0,
    )
    h_pair = split(h_all)
    h_low = split(joined(dot(h_pair, adapter_ref[...], NT)))
    quarter = m * SH + half + t0 * Q
    parts = []
    for i in range(QB):
        q = quarter // R + i
        part = joined(dot(h_pair, wq[i], NT)) + joined(dot(h_low, at[q // MP, q % MP]))
        parts.append(part * gain_ref[:, pl.ds(pl.multiple_of(quarter + i * R, 128), R)].astype(F32))
    result = jnp.concatenate(parts, axis=1)
    for i in range(1, DP):
        landed(s2r.at[(e + DP - i) % DP], s2_ss.at[i], s2_rs.at[i])
    for i in range(DP):
        result = result - s2r[i].astype(F32)
    fo[...] = result
    UH = UN // 2
    f_core = u // UH
    f_unit = u % UH
    f_cols = pl.ds(pl.multiple_of(half + t0 * Q, 128), Q)
    f_there = out_enc.at[pl.ds(pl.multiple_of(f_unit * RU, 8), RU), f_cols]
    for i in range(1, DP):
        send(fo, f_there, fo_ss.at[i], fo_rs.at[f_unit, p, c], dp=(e + i) % DP, grp=f_core)
    f_away = copy(fo, f_there, fo_ss.at[0], fo_rs.at[f_unit, p, c], grp=oc)

    @pl.when(f_core == c)
    def _():
        out_enc[pl.ds(pl.multiple_of(f_unit * RU, 8), RU), f_cols] = fo[...]

    @pl.when(f_core != c)
    def _():
        f_away.start()

    for i in range(DH):
        for j in range(MP):
            for k in range(2):
                other = copy(yos, out_llm.at[i, :, pl.ds(k * KH + j * NB, NB)], yo_ss.at[0], yo_rs.at[i, j, k], grp=oc)

                @pl.when(jnp.logical_not((y_core == c) & (y_row == i) & (m == j) & (c == k)))
                def _():
                    other.wait_recv()

    for i in range(UH):
        for j in range(2):
            for k in range(2):
                t_other = (j + m // 2 + k) % 2
                cols = pl.ds(pl.multiple_of(k * HC + t_other * Q, 128), Q)
                arrival = copy(fo, out_enc.at[pl.ds(i * RU, RU), cols], fo_ss.at[0], fo_rs.at[i, j, k], grp=oc)

                @pl.when(jnp.logical_not((f_core == c) & (f_unit == i) & (p == j) & (c == k)))
                def _():
                    arrival.wait_recv()

    for one in pending:
        one.wait_send()
    for started, one in w_sends:

        @pl.when(started)
        def _():
            one.wait_send()

    @pl.when(y_core != c)
    def _():
        y_away.wait_send()

    @pl.when(f_core != c)
    def _():
        f_away.wait_send()


def body(
    hidden, enc_weight, enc_bias, enc_frozen, enc_adapter, text_rows, norm_gain, value_weight,
    value_bias, llm_frozen, llm_adapter, targets, dest_owner, seq_length,
):
    DP, MP = lax.axis_size("dp"), lax.axis_size("mp")
    OWN = DP * MP
    NTOK, MH = hidden.shape
    BT = NTOK * MP
    LR, D = text_rows.shape
    RANK = enc_frozen.shape[1]
    KV = llm_adapter.shape[1]
    CAP = 2 * BT // OWN
    ST = CAP + 8
    ST = ST + -ST % 16
    SH = enc_weight.shape[1]
    HC, Q = SH // 2, SH // 4
    R = value_weight.shape[0]
    UN = DP // 2
    RU, RD, RG = RANK // UN, RANK // DP, RANK // 2
    KH, NB = KV // 2, KV // (2 * MP)
    KC = 1024 if MH % 1024 == 0 else MH
    NK = MH // KC
    QB = Q // R
    RL = RANK + 8
    sizes = dict(
        DP=DP, MP=MP, NTOK=NTOK, BT=BT, CAP=CAP, ST=ST, LR=LR, D=D, MH=MH, RANK=RANK, KV=KV, NB=NB,
        SH=SH, HC=HC, Q=Q, R=R, UN=UN, RU=RU, RD=RD, RG=RG, KC=KC,
    )
    vmem = pl.BlockSpec(memory_space=pltpu.VMEM)
    hbm = pl.BlockSpec(memory_space=pl.ANY)
    V = pltpu.VMEM
    S = pltpu.SemaphoreType.DMA
    scratch = [
        V((MH, HC), BF16), V((BT, MH), BF16), V((BT, HC), F32), V((BT, RANK), F32), V((BT, HC), BF16),
        V((2, BT, Q), BF16), V((BT, Q), BF16), V((QB, R, KV), BF16), V((DP, MP, RANK, R), BF16), V((LR, D), BF16),
        V((MP, 2, RANK, Q), BF16), V((2, MP, RANK, Q), BF16), V((DP, MP, ST, NB), BF16), V((DP, MP, ST, NB), BF16),
        V((RL, BT), F32), V((2 * MP, RL, BT), F32),
        V((2, BT, KH), F32), V((2, BT, KH), BF16), V((2, BT, KH), BF16),
        V((2, MP, BT, NB), BF16), V((2, MP, BT, NB), BF16),
        V((RANK, KH), F32), V((RANK, KH), F32), V((DP, MP, RD, NB), F32), V((DP, MP, RD, NB), F32),
        V((8, BT), F32), V((2 * MP, 8, BT), F32), V((DP, 2, RD, NB), F32), V((DP, 2, RD, NB), F32),
        V((RD, NB), F32), V((2, 2, MP, RD, NB), F32), V((RD, NB), F32),
        V((2, UN, RU, Q), BF16), V((DP, RU, Q), BF16), V((RU, Q), F32),
        S((NK,)), S(()), S(()), S((NK, MP)), S((NK, MP)), S((NK, MP)), S((NK, MP)),
        S(((UN + 1) // 2,)), S((QB,)), S((DP,)), S((DP,)), S((MP,)), S((MP,)),
        S(()), S(()), S((OWN,)), S((OWN,)), S(()), S(()), S((2 * MP,)), S((2 * MP,)), S((2 * MP,)), S((2 * MP,)),
        S((2,)), S((2,)), S((2 * MP,)), S((2 * MP,)),
        S(()), S(()), S((OWN,)), S((OWN,)), S((2 * MP,)), S((2 * MP,)), S((DP,)), S((DP,)),
        S((4 * MP,)), S((4 * MP,)), S((OWN,)), S((DP // 2, MP, 2)),
        S((DP,)), S((DP,)), S((DP,)), S((UN // 2, 2, 2)),
    ]
    grad_enc, grad_llm = pl.pallas_call(
        functools.partial(kernel, sizes),
        out_shape=(
            jax.ShapeDtypeStruct((RG, SH), F32),
            jax.ShapeDtypeStruct((DP // 2, RD, KV), F32),
        ),
        in_specs=[hbm, hbm, vmem, vmem, vmem, hbm, vmem, hbm, vmem, vmem, vmem, vmem, vmem, vmem],
        out_specs=(vmem, vmem),
        scratch_shapes=scratch,
        compiler_params=pltpu.CompilerParams(
            collective_id=0, has_side_effects=True, vmem_limit_bytes=60 * 1024 * 1024
        ),
    )(
        hidden, enc_weight, enc_bias.reshape(1, SH), enc_frozen, enc_adapter, text_rows,
        norm_gain.reshape(1, D), value_weight, value_bias.reshape(1, KV), llm_frozen, llm_adapter,
        targets, dest_owner, seq_length.reshape(1, 1),
    )
    return grad_enc, grad_llm.reshape(RG, KV)


def solution(mesh):
    return jax.shard_map(
        body,
        mesh=mesh,
        in_specs=(
            P(("dp", "mp"), None), P(None, "mp"), P("mp"), P(), P(None, "mp"), P(("dp", "mp"), None), P(),
            P(("dp", "mp"), None), P(), P(("dp", "mp"), None), P(), P(("dp", "mp"), None), P(), P(("dp", "mp")),
        ),
        out_specs=(P("grp", "mp"), P("grp", None)),
        check_vma=False,
    )
```

time: 259 us -> 105 us (0.41)
  waiting for transfers between devices: 126 us -> 0 us
  Pallas kernels: 0 us -> 90.4 us
  blocking collectives: 58.1 us -> 0 us
  matrix products: 20.1 us -> 0 us
  starting transfers between devices: 16.5 us -> 0 us
  other arithmetic: 16.1 us -> 0 us
  between operations: 15.3 us -> 1.29 us
  local copies, waits for them, and re-layouts: 5.9 us -> 12.8 us
    pallas_call x0 -> x1, Pallas kernels: none -> 90.4 us  [body(): pl.pallas_call(functools.partial(kernel, sizes), out_shape=(jax.ShapeDtyp...]
    all_gather x2 -> x0, waiting for transfers between devices: 63.7 us -> none  [the longest x1 33.7 us: body(): weights = lax.all_gather(packed, ('dp', 'mp'), axis=0, tiled=True)]
    ppermute x10 -> x0, waiting for transfers between devices: 44.1 us -> none  [swapped(): lax.ppermute(array, axis, [(i, i ^ 1 << bit) for i in range(lax.axis_size...]
    unnamed x1 -> x0, blocking collectives: 42.1 us -> none
    dot_general x10 -> x0, matrix products: 20.1 us -> none  [the longest x1 7.93 us: body(): product = jnp.dot(normed, weights, preferred_element_type=F32)]
    all_to_all x3 -> x0, waiting for transfers between devices: 18.5 us -> none  [the longest x1 9.57 us: body(): head = lax.all_to_all(head, 'dp', split_axis=1, concat_axis=1, tiled=True)]
    all_gather x1 -> x0, blocking collectives: 16 us -> none  [body(): table = lax.all_gather(head, 'mp', axis=0, tiled=False)]
    all_to_all x3 -> x0, starting transfers between devices: 10.3 us -> none  [the longest x1 3.47 us: body(): back = lax.all_to_all(dimage, 'mp', split_axis=0, concat_axis=0, tiled=True)]
  transfers between devices with their start and end apart: 15 -> 0, of which waited for: 12 -> 0; matrix products, arithmetic and copies ran while one was open for 9% -> 0% of each run, Pallas kernels for 0% -> 0%
where the time goes in v1:
time: 105 us; the launch traced here: 104 us
  Pallas kernels  90.4 us (86%)
  local copies, waits for them, and re-layouts  12.8 us (12%)
  between operations  1.29 us (1%)
    pallas_call x1, Pallas kernels, body(): pl.pallas_call(functools.partial(kernel, sizes), out_shape=(jax.ShapeDtyp...  90.4 us
    unnamed x5, local copies, waits for them, and re-layouts  8.9 us

profile of v1, /device:TPU:0, one launch (start us, length us, event | category | flops | bytes accessed | tf_op | source)
XLA Modules:
  0.0 104.5 jit_solution(7388952511673197325)
XLA Ops:
  1.3 1.3 %reshape.21.bias_ref = bf16[1,1024]{1,0:T(2,128)(2,1)} reshape(bf16[1024]{0:T(1024)(128)(2,1)} %param.22) | data formatting | bytes 4096 | tf_op jit(solution)/shard_map/reshape | solution.py:612
  2.6 1.3 %reshape.19.enc_bias = bf16[1,2048]{1,0:T(2,128)(2,1)} reshape(bf16[2048]{0:T(1024)(128)(2,1)} %param.16) | data formatting | bytes 8192 | tf_op jit(solution)/shard_map/reshape | solution.py:611
  3.8 1.3 %reshape.20.gain_ref = bf16[1,8192]{1,0:T(2,128)(2,1)} reshape(bf16[8192]{0:T(1024)(128)(2,1)} %param.20) | data formatting | bytes 32768 | tf_op jit(solution)/shard_map/reshape | solution.py:612
  5.2 1.6 %copy.17.llm_frozen = bf16[512,64]{1,0:T(8,128)(2,1)} copy(bf16[512,64]{0,1:T(8,128)(2,1)} %param.23) | data formatting | bytes 131072 | tf_op args[9]
  6.8 1.7 %copy.18.dest = s32[1024,1]{1,0:T(8,128)} copy(s32[1024,1]{0,1:T(1,128)} %param.26) | data formatting | bytes 8192 | tf_op args[12]
  8.5 2.3 %copy.16.enc_frozen = bf16[5120,64]{1,0:T(8,128)(2,1)} copy(bf16[5120,64]{0,1:T(8,128)(2,1)} %param.17) | data formatting | bytes 1310720 | tf_op args[3]
  10.9 90.4 %shard_map.149 = (f32[32,2048]{1,0:T(8,128)}, f32[2,16,1024]{2,1,0:T(8,128)}) custom-call(bf16[64,5120]{1,0:T(8,128)(2,1)} %hidden.1, bf16[5120,2048]{1,0:T(8,128)(2,1)} %enc_weight.1, bf16[1,2048]{1,0:T(2,128)(2,1)} %reshape.19.enc_bias, bf16[5120,64]{1,0:T(8,128)(2,1)} %copy.16.enc_frozen, bf16[64,2048]{1,0:T(8,128)(2,1)} %enc_adapter.1, ...), custom_call_target="tpu_custom_call" | custom-call | tf_op jit(solution)/shard_map/pallas_call | solution.py:598
  101.2 1.7 %copy.22 = f32[32,2048]{1,0:T(8,128)} copy(f32[32,2048]{1,0:T(8,128)} %get-tuple-element.8) | data formatting | bytes 524288
  102.9 1.6 %copy.23 = f32[32,1024]{1,0:T(8,128)} copy(f32[32,1024]{1,0:T(8,128)} %bitcast.3) | data formatting | bytes 262144

commit v2 on v1

--- a/solution.py
+++ b/solution.py
@@ -38,12 +38,12 @@
 
 def kernel(
     sizes,
-    hidden, enc_weight, enc_bias, enc_frozen, enc_adapter, text_rows, gain_ref, value_weight,
-    bias_ref, llm_frozen, adapter_ref, targets, dest, seq_length,
+    hidden, enc_weight, enc_bias_in, enc_frozen, enc_adapter, text_rows, gain_in, value_weight,
+    bias_in, llm_frozen, adapter_ref, targets, dest, seq_length,
     out_enc, out_llm,
-    ebuf, hid, acc, acc_low, img, xq, xr, wq, at, txt, gs, gr, tgs, tgr, los, lor,
-    vown, vps, vpr, vs, vr, ys, yr, yrs, yrr, ss, sr, hys, hyr, hbs, hb, yos, s2s, s2r, fo,
-    e_sem, t_sem, own_sem, h_ss, h_rs, hf_ss, hf_rs, w_ss, w_rs, a1_ss, a1_rs, a2_ss, a2_rs,
+    gain_ref, enc_bias, bias_ref, ebuf, hid, acc, acc_low, img, xq, xr, wq, at, txt, gs, gr, tgs, tgr, los, lor,
+    vown, vps, vpr, vs, vr, lop, ys, yr, yrs, yrr, ss, sr, hys, hyr, hbs, hb, yos, s2s, s2r, fo, fin,
+    e_sem, t_sem, own_sem, h_ss, h_rs, hf_ss, hf_rs, w_ss, w_rs, lp_ss, lp_rs, a1_ss, a1_rs, a2_ss, a2_rs,
     a3_ss, a3_rs, tg_ss, tg_rs, x_ss, x_rs, lo_ss, lo_rs, g_ss, g_rs, vp_ss, vp_rs, v_ss, v_rs,
     yp_ss, yp_rs, yr_ss, yr_rs, s_ss, s_rs, hy_ss, hy_rs, hb_ss, hb_rs, yo_ss, yo_rs,
     s2_ss, s2_rs, fo_ss, fo_rs,
@@ -80,6 +80,18 @@
     def landed(dst, ssem, rsem):
         copy(dst, dst, ssem, rsem, grp=oc).wait_recv()
 
+    barrier = pltpu.get_barrier_semaphore()
+    devices = 2 * OWN
+    place = (c * DP + e) * MP + m
+
+    def greet(i, carry):
+        other = (place + i) % devices
+        device = {"grp": other // OWN, "dp": other // MP % DP, "mp": other % MP}
+        pl.semaphore_signal(barrier, inc=1, device_id=device, device_id_type=MESH)
+        return carry
+
+    lax.fori_loop(1, devices, greet, 0)
+
     half = c * HC
     loads = []
     for k in range(NK):
@@ -96,8 +108,11 @@
 
     RH = RANK // 2
     low_half = c * RH
-    at_own = dot(eye(RANK), llm_frozen[...], NT).astype(BF16)
-    at[e, m, pl.ds(low_half, RH), :] = jnp.where(c == 0, at_own[:RH], at_own[RH:])
+    at[e, m, pl.ds(low_half, RH), :] = llm_frozen[pl.ds(pl.multiple_of(low_half, 16), RH), :]
+    for packed, row in ((gain_in, gain_ref), (enc_bias_in, enc_bias), (bias_in, bias_ref)):
+        wide = packed[...].astype(F32)
+        for i in range(wide.shape[0]):
+            row[:, i * 128 : (i + 1) * 128] = wide[i : i + 1]
     rows = CAP * DP
     order_i = lax.broadcasted_iota(jnp.int32, (rows, rows), 0)
     order_j = lax.broadcasted_iota(jnp.int32, (rows, rows), 1)
@@ -110,18 +125,33 @@
             tail = jnp.broadcast_to(length, (ST - CAP, NB)).astype(BF16)
             tgs[i, j] = jnp.concatenate([block, tail], axis=0)
 
-    barrier = pltpu.get_barrier_semaphore()
-    devices = 2 * OWN
-    place = (c * DP + e) * MP + m
-
-    def greet(i, carry):
-        other = (place + i) % devices
-        device = {"grp": other // OWN, "dp": other // MP % DP, "mp": other % MP}
-        pl.semaphore_signal(barrier, inc=1, device_id=device, device_id_type=MESH)
-        return carry
-
-    lax.fori_loop(1, devices, greet, 0)
     pl.semaphore_wait(barrier, devices - 1)
+
+    w_sends = []
+
+    def send_weights():
+        w_row = owner * R
+        w_m = w_row // SH
+        w_t = w_row % SH // Q
+        w_slot = w_row % Q // R
+        w_core = w_t // 2
+        w_par = (w_t % 2 + w_t // 2 + w_m // 2) % 2
+        for i in range((UN + 1) // 2):
+            w_u = 2 * i + c
+            there = 2 * w_u + w_par
+            self_case = (there == e) & (w_m == m) & (w_core == c)
+            live = w_u < UN
+            away = copy(value_weight, wq.at[w_slot], w_ss.at[i], w_rs.at[w_slot], dp=there, mp=w_m, grp=w_core)
+            near = pltpu.make_async_copy(value_weight, wq.at[w_slot], w_rs.at[w_slot])
+            w_sends.append((live & jnp.logical_not(self_case), away))
+
+            @pl.when(live & jnp.logical_not(self_case))
+            def _():
+                away.start()
+
+            @pl.when(live & self_case)
+            def _():
+                near.start()
 
     for i in range(1, DP):
         mine = at.at[e, m, pl.ds(low_half, RH), :]
@@ -132,30 +162,7 @@
         cols = pl.ds(k * KC, KC)
         for i in range(1, MP):
             send(hidden.at[pl.ds(c * NH, NH), cols], hid.at[hid_rows, cols], h_ss.at[k, i], h_rs.at[k, i], mp=(m + i) % MP)
-    w_row = owner * R
-    w_m = w_row // SH
-    w_t = w_row % SH // Q
-    w_slot = w_row % Q // R
-    w_core = w_t // 2
-    w_par = (w_t % 2 + w_t // 2 + w_m // 2) % 2
-    w_sends = []
-    for i in range((UN + 1) // 2):
-        w_u = 2 * i + c
-        there = 2 * w_u + w_par
-        self_case = (there == e) & (w_m == m) & (w_core == c)
-        live = w_u < UN
-        away = copy(value_weight, wq.at[w_slot], w_ss.at[i], w_rs.at[w_slot], dp=there, mp=w_m, grp=w_core)
-        near = pltpu.make_async_copy(value_weight, wq.at[w_slot], w_rs.at[w_slot])
-        w_sends.append((live & jnp.logical_not(self_case), away))
-
-        @pl.when(live & jnp.logical_not(self_case))
-        def _():
-            away.start()
-
-        @pl.when(live & self_case)
-        def _():
-            near.start()
-
+    send_weights()
     for i in range(1, OWN):
         other = (owner + i) % OWN
         od, om = other // MP, other % MP
@@ -177,7 +184,7 @@
         inverse = lax.rsqrt(jnp.sum(total, axis=1, keepdims=True) / D + epsilon)
         for k in range(D // CW):
             cols = pl.ds(k * CW, CW)
-            txt[r, cols] = (txt[r, cols].astype(F32) * inverse * gain_ref[:, cols].astype(F32)).astype(BF16)
+            txt[r, cols] = (txt[r, cols].astype(F32) * inverse * gain_ref[:, cols]).astype(BF16)
         return carry
 
     lax.fori_loop(0, LR // TR, text_norm, 0)
@@ -213,7 +220,7 @@
             return carry
 
         lax.fori_loop(0, HC // TN, product, 0)
-        low_part = dot(hid[:, cols], enc_frozen[cols, :])
+        low_part = dot(hid[:, cols], enc_frozen[:, cols], NT)
         if k == 0:
             acc_low[...] = low_part
         else:
@@ -224,14 +231,14 @@
     for n in range(HC // TN):
         cols = pl.ds(n * TN, TN)
         shifted = pl.ds(half + n * TN, TN)
-        merged = acc[:, cols] + enc_bias[:, shifted].astype(F32) + dot(enc_low, enc_adapter[:, shifted])
+        merged = acc[:, cols] + enc_bias[:, shifted] + dot(enc_low, enc_adapter[:, shifted])
         merged = merged.astype(BF16)
         img[:, cols] = merged
         wide = merged.astype(F32)
         square = wide * wide
         for i in range(TN // 128):
             squares = squares + square[:, i * 128 : (i + 1) * 128]
-        scaled = (wide * gain_ref[:, pl.ds(m * SH + half + n * TN, TN)].astype(F32)).astype(BF16)
+        scaled = (wide * gain_ref[:, pl.ds(m * SH + half + n * TN, TN)]).astype(BF16)
         xq[n * TN // Q, :, n * TN % Q : n * TN % Q + TN] = scaled
     pair = e + 1 - 2 * p
     send(xq.at[1 - t0], xr, x_ss, x_rs, dp=pair)
@@ -252,31 +259,29 @@
     total = jnp.broadcast_to(jnp.sum(squares, axis=1, keepdims=True), (BT, 128))
     los[...] = jnp.concatenate([low_part, total.T[:8]], axis=0)
     me8 = m * 2 + c
-    for i in range(1, 2 * MP):
-        other = (me8 + i) % (2 * MP)
-        send(los, lor.at[me8], lo_ss.at[i], lo_rs.at[i], mp=other // 2, grp=other % 2)
-    lor[me8] = los[...]
+    send(los, lop, lp_ss, lp_rs, grp=oc)
+    landed(lop, lp_ss, lp_rs)
+    lor[m] = los[...] + lop[...]
+    for i in range(1, MP):
+        send(lor.at[m], lor.at[m], lo_ss.at[i], lo_rs.at[i], mp=(m + i) % MP)
 
     def text_low(q, carry):
-        lt, ln = carry
         part = txt[:, pl.ds(pl.multiple_of(q * R, 128), R)]
-        a = at[q // MP, q % MP]
-        return lt + dot(a, part, NT), ln + dot(part, a, NT)
-
-    text_low_t, text_low_n = lax.fori_loop(
-        0, OWN, text_low, (jnp.zeros((RANK, LR), F32), jnp.zeros((LR, RANK), F32))
-    )
+        return carry + dot(part, at[q // MP, q % MP], NT)
+
+    text_low_n = lax.fori_loop(0, OWN, text_low, jnp.zeros((LR, RANK), F32))
+    text_low_b = text_low_n.astype(BF16)
+    text_low_t = jnp.concatenate([text_low_b.astype(F32), jnp.zeros((LR, 128 - RANK), F32)], axis=1).T[:RANK]
     place_row = lax.broadcasted_iota(jnp.int32, (8, LR), 1)
     count = jnp.zeros((8, LR), F32)
     for i in range(DP):
-        named = (dest[pl.ds(i * BT, BT), :] == owner).astype(F32)
-        named = jnp.sum(named, axis=0, keepdims=True)
+        named = (dest[:, i * BT : (i + 1) * BT] == owner).astype(F32)
+        named = jnp.sum(named, axis=1, keepdims=True)
         count = jnp.where(place_row % DP == i, jnp.broadcast_to(named, (8, LR)), count)
     replaced = (place_row < CAP * DP) & ((place_row // DP).astype(F32) < count)
     live = (place_row.astype(F32) < jnp.broadcast_to(length, (8, LR))) & jnp.logical_not(replaced)
     live = jnp.where(live, 1.0, 0.0)[:1]
-    text_low_m = (text_low_t.astype(BF16).astype(F32) * live).astype(BF16)
-    text_low_b = text_low_n.astype(BF16)
+    text_low_m = (text_low_t * live).astype(BF16)
     scale = 1.0 / length
     here8 = p * MP + m
     for j in range(MP):
@@ -289,40 +294,10 @@
         send(gs.at[gm, (gp + gm // 2 + c) % 2], gr.at[p, m], g_ss.at[i], g_rs.at[i], dp=2 * u + gp, mp=gm)
     gr[p, m] = gs[m, t0]
     text_y = dot(text_low_b, adapter_ref[:, pl.ds(c * KH, KH)])
-    text_y = text_y + bias_ref[:, pl.ds(c * KH, KH)].astype(F32) - targets[:, pl.ds(c * KH, KH)].astype(F32)
+    text_y = text_y + bias_ref[:, pl.ds(c * KH, KH)] - targets[:, pl.ds(c * KH, KH)].astype(F32)
     high = text_y.astype(BF16)
     rest = (text_y - high.astype(F32)).astype(BF16)
     text_grad = (dot(text_low_m, high) + dot(text_low_m, rest)) * scale
-
-    for i in range(1, OWN):
-        other = (owner + OWN - i) % OWN
-        landed(tgr.at[other // MP, other % MP], tg_ss.at[i], tg_rs.at[i])
-    block_dest = dest[pl.ds(pl.multiple_of(e * BT, 8), BT), :]
-    marks = block_dest == lax.broadcasted_iota(jnp.int32, (BT, 128), 1)
-    before = lax.broadcasted_iota(jnp.int32, (BT, BT), 0) > lax.broadcasted_iota(jnp.int32, (BT, BT), 1)
-    counted = dot(before.astype(BF16), marks.astype(BF16))
-    slot = jnp.sum(jnp.where(marks, counted, 0.0), axis=1, keepdims=True)
-    base = block_dest.astype(F32) * ST
-    table_rows = lax.broadcasted_iota(jnp.int32, (BT, OWN * ST), 1).astype(F32)
-    table = tgr[...].reshape(OWN * ST, NB)
-    image_targets = dot((table_rows == base + slot).astype(BF16), table)
-    image_length = dot((table_rows == base + CAP).astype(BF16), table)
-    position = slot * DP + e.astype(F32)
-    weight = jnp.where(position < image_length, 1.0 / image_length, 0.0)
-
-    gathered = jnp.zeros((RANK + 8, BT), F32)
-    for i in range(1, 2 * MP):
-        other = (me8 + 2 * MP - i) % (2 * MP)
-        landed(lor.at[other], lo_ss.at[i], lo_rs.at[i])
-    for i in range(2 * MP):
-        gathered = gathered + lor[i]
-    inverse_row = lax.rsqrt(gathered[RANK : RANK + 1] / D + epsilon)
-    low_t = (gathered[:RANK] * inverse_row).astype(BF16)
-    turned = jnp.concatenate(
-        [low_t.astype(F32), jnp.broadcast_to(inverse_row, (128 - RANK, BT))], axis=0
-    ).T
-    low = turned[:, :RANK].astype(BF16)
-    inverse = turned[:, RANK : RANK + 1]
 
     for i in range(QB):
         landed(wq.at[i], w_ss.at[0], w_rs.at[i])
@@ -354,6 +329,63 @@
         send(vs.at[gp, gm], vr.at[p, m], v_ss.at[i], v_rs.at[i], dp=2 * u + gp, mp=gm)
     vr[p, m] = vs[p, m]
 
+    for i in range(1, OWN):
+        other = (owner + OWN - i) % OWN
+        landed(tgr.at[other // MP, other % MP], tg_ss.at[i], tg_rs.at[i])
+    block_dest = dest[:, pl.ds(pl.multiple_of(e * BT, 128), BT)].astype(F32)
+    block_dest = jnp.broadcast_to(block_dest, (128, BT)).T
+    marks = block_dest == lax.broadcasted_iota(jnp.int32, (BT, 128), 1).astype(F32)
+    before = lax.broadcasted_iota(jnp.int32, (BT, BT), 0) > lax.broadcasted_iota(jnp.int32, (BT, BT), 1)
+    counted = dot(before.astype(BF16), marks.astype(BF16))
+    slot = jnp.sum(jnp.where(marks, counted, 0.0), axis=1, keepdims=True)
+    base = block_dest[:, :1] * ST
+    table_rows = lax.broadcasted_iota(jnp.int32, (BT, OWN * ST), 1).astype(F32)
+    table = tgr[...].reshape(OWN * ST, NB)
+    image_targets = dot((table_rows == base + slot).astype(BF16), table)
+    image_length = dot((table_rows == base + CAP).astype(BF16), table)
+    position = slot * DP + e.astype(F32)
+    weight = jnp.where(position < image_length, 1.0 / image_length, 0.0)
+
+    gathered = jnp.zeros((RANK + 8, BT), F32)
+    for i in range(1, MP):
+        landed(lor.at[(m + MP - i) % MP], lo_ss.at[i], lo_rs.at[i])
+    for i in range(MP):
+        gathered = gathered + lor[i]
+    inverse_row = lax.rsqrt(gathered[RANK : RANK + 1] / D + epsilon)
+    low_t = (gathered[:RANK] * inverse_row).astype(BF16)
+    turned = jnp.concatenate(
+        [low_t.astype(F32), jnp.broadcast_to(inverse_row, (128 - RANK, BT))], axis=0
+    ).T
+    low = turned[:, :RANK].astype(BF16)
+    inverse = turned[:, RANK : RANK + 1]
+
+    for i in range(1, 2 * MP):
+        other = (here8 + 2 * MP - i) % (2 * MP)
+        landed(vr.at[other // MP, other % MP], v_ss.at[i], v_rs.at[i])
+    product_sum = jnp.zeros((BT, NB), F32)
+    for i in range(2):
+        for j in range(MP):
+            product_sum = product_sum + vr[i, j].astype(F32)
+    own_cols = pl.ds(pl.multiple_of(c * KH + m * NB, 128), NB)
+    plain = product_sum * inverse + dot(low, adapter_ref[:, own_cols])
+    dv = plain + bias_ref[:, own_cols] - image_targets
+    dv = (dv * weight).astype(BF16)
+    along = jnp.sum(dv.astype(F32) * plain, axis=1, keepdims=True)
+    ss[...] = jnp.broadcast_to(along, (BT, 128)).T[:8]
+    for i in range(1, 2 * MP):
+        other = (me8 + i) % (2 * MP)
+        send(ss, sr.at[me8], s_ss.at[i], s_rs.at[i], mp=other // 2, grp=other % 2)
+    sr[me8] = ss[...]
+    h_part = joined(dot(split(enc_low_t * inverse_row), dv))
+    y_part = dot(low_t, dv)
+    for i in range(DP):
+        hys[i, 0] = h_part[i * RD : (i + 1) * RD]
+        hys[i, 1] = y_part[i * RD : (i + 1) * RD]
+    for i in range(1, DP):
+        there = (e + i) % DP
+        send(hys.at[there], hyr.at[e], hy_ss.at[i], hy_rs.at[i], dp=there)
+    hyr[e] = hys[e]
+
     for i in range(1, 2 * MP):
         other = (here8 + 2 * MP - i) % (2 * MP)
         landed(gr.at[other // MP, other % MP], g_ss.at[i], g_rs.at[i])
@@ -382,33 +414,6 @@
         od, om = other // MP, other % MP
         send(yrs.at[od, om], yrr.at[e, m], yr_ss.at[i], yr_rs.at[i], dp=od, mp=om)
     yrr[e, m] = yrs[e, m]
-
-    for i in range(1, 2 * MP):
-        other = (here8 + 2 * MP - i) % (2 * MP)
-        landed(vr.at[other // MP, other % MP], v_ss.at[i], v_rs.at[i])
-    product_sum = jnp.zeros((BT, NB), F32)
-    for i in range(2):
-        for j in range(MP):
-            product_sum = product_sum + vr[i, j].astype(F32)
-    own_cols = pl.ds(pl.multiple_of(c * KH + m * NB, 128), NB)
-    plain = product_sum * inverse + dot(low, adapter_ref[:, own_cols])
-    dv = plain + bias_ref[:, own_cols].astype(F32) - image_targets
-    dv = (dv * weight).astype(BF16)
-    along = jnp.sum(dv.astype(F32) * plain, axis=1, keepdims=True)
-    ss[...] = jnp.broadcast_to(along, (BT, 128)).T[:8]
-    for i in range(1, 2 * MP):
-        other = (me8 + i) % (2 * MP)
-        send(ss, sr.at[me8], s_ss.at[i], s_rs.at[i], mp=other // 2, grp=other % 2)
-    sr[me8] = ss[...]
-    h_part = joined(dot(split(enc_low_t * inverse_row), dv))
-    y_part = dot(low_t, dv)
-    for i in range(DP):
-        hys[i, 0] = h_part[i * RD : (i + 1) * RD]
-        hys[i, 1] = y_part[i * RD : (i + 1) * RD]
-    for i in range(1, DP):
-        there = (e + i) % DP
-        send(hys.at[there], hyr.at[e], hy_ss.at[i], hy_rs.at[i], dp=there)
-    hyr[e] = hys[e]
 
     for i in range(1, 2 * MP):
         other = (me8 + 2 * MP - i) % (2 * MP)
@@ -483,25 +488,24 @@
     for i in range(QB):
         q = quarter // R + i
         part = joined(dot(h_pair, wq[i], NT)) + joined(dot(h_low, at[q // MP, q % MP]))
-        parts.append(part * gain_ref[:, pl.ds(pl.multiple_of(quarter + i * R, 128), R)].astype(F32))
+        parts.append(part * gain_ref[:, pl.ds(pl.multiple_of(quarter + i * R, 128), R)])
     result = jnp.concatenate(parts, axis=1)
     for i in range(1, DP):
         landed(s2r.at[(e + DP - i) % DP], s2_ss.at[i], s2_rs.at[i])
     for i in range(DP):
         result = result - s2r[i].astype(F32)
-    fo[...] = result
+    fo[...] = result.astype(BF16)
     UH = UN // 2
     f_core = u // UH
     f_unit = u % UH
-    f_cols = pl.ds(pl.multiple_of(half + t0 * Q, 128), Q)
-    f_there = out_enc.at[pl.ds(pl.multiple_of(f_unit * RU, 8), RU), f_cols]
+    f_there = fin.at[f_unit, p, c]
     for i in range(1, DP):
         send(fo, f_there, fo_ss.at[i], fo_rs.at[f_unit, p, c], dp=(e + i) % DP, grp=f_core)
     f_away = copy(fo, f_there, fo_ss.at[0], fo_rs.at[f_unit, p, c], grp=oc)
 
     @pl.when(f_core == c)
     def _():
-        out_enc[pl.ds(pl.multiple_of(f_unit * RU, 8), RU), f_cols] = fo[...]
+        fin[f_unit, p, c] = fo[...]
 
     @pl.when(f_core != c)
     def _():
@@ -521,11 +525,13 @@
             for k in range(2):
                 t_other = (j + m // 2 + k) % 2
                 cols = pl.ds(pl.multiple_of(k * HC + t_other * Q, 128), Q)
-                arrival = copy(fo, out_enc.at[pl.ds(i * RU, RU), cols], fo_ss.at[0], fo_rs.at[i, j, k], grp=oc)
+                arrival = copy(fo, fin.at[i, j, k], fo_ss.at[0], fo_rs.at[i, j, k], grp=oc)
 
                 @pl.when(jnp.logical_not((f_core == c) & (f_unit == i) & (p == j) & (c == k)))
                 def _():
                     arrival.wait_recv()
+
+                out_enc[pl.ds(i * RU, RU), cols] = fin[i, j, k].astype(F32)
 
     for one in pending:
         one.wait_send()
@@ -577,18 +583,20 @@
     V = pltpu.VMEM
     S = pltpu.SemaphoreType.DMA
     scratch = [
+        V((1, D), F32), V((1, SH), F32), V((1, KV), F32),
         V((MH, HC), BF16), V((BT, MH), BF16), V((BT, HC), F32), V((BT, RANK), F32), V((BT, HC), BF16),
         V((2, BT, Q), BF16), V((BT, Q), BF16), V((QB, R, KV), BF16), V((DP, MP, RANK, R), BF16), V((LR, D), BF16),
         V((MP, 2, RANK, Q), BF16), V((2, MP, RANK, Q), BF16), V((DP, MP, ST, NB), BF16), V((DP, MP, ST, NB), BF16),
-        V((RL, BT), F32), V((2 * MP, RL, BT), F32),
+        V((RL, BT), F32), V((MP, RL, BT), F32),
         V((2, BT, KH), F32), V((2, BT, KH), BF16), V((2, BT, KH), BF16),
         V((2, MP, BT, NB), BF16), V((2, MP, BT, NB), BF16),
+        V((RL, BT), F32),
         V((RANK, KH), F32), V((RANK, KH), F32), V((DP, MP, RD, NB), F32), V((DP, MP, RD, NB), F32),
         V((8, BT), F32), V((2 * MP, 8, BT), F32), V((DP, 2, RD, NB), F32), V((DP, 2, RD, NB), F32),
         V((RD, NB), F32), V((2, 2, MP, RD, NB), F32), V((RD, NB), F32),
-        V((2, UN, RU, Q), BF16), V((DP, RU, Q), BF16), V((RU, Q), F32),
+        V((2, UN, RU, Q), BF16), V((DP, RU, Q), BF16), V((RU, Q), BF16), V((UN // 2, 2, 2, RU, Q), BF16),
         S((NK,)), S(()), S(()), S((NK, MP)), S((NK, MP)), S((NK, MP)), S((NK, MP)),
-        S(((UN + 1) // 2,)), S((QB,)), S((DP,)), S((DP,)), S((MP,)), S((MP,)),
+        S(((UN + 1) // 2,)), S((QB,)), S(()), S(()), S((DP,)), S((DP,)), S((MP,)), S((MP,)),
         S(()), S(()), S((OWN,)), S((OWN,)), S(()), S(()), S((2 * MP,)), S((2 * MP,)), S((2 * MP,)), S((2 * MP,)),
         S((2,)), S((2,)), S((2 * MP,)), S((2 * MP,)),
         S(()), S(()), S((OWN,)), S((OWN,)), S((2 * MP,)), S((2 * MP,)), S((DP,)), S((DP,)),
@@ -608,9 +616,9 @@
             collective_id=0, has_side_effects=True, vmem_limit_bytes=60 * 1024 * 1024
         ),
     )(
-        hidden, enc_weight, enc_bias.reshape(1, SH), enc_frozen, enc_adapter, text_rows,
-        norm_gain.reshape(1, D), value_weight, value_bias.reshape(1, KV), llm_frozen, llm_adapter,
-        targets, dest_owner, seq_length.reshape(1, 1),
+        hidden, enc_weight, enc_bias.reshape(-1, 128), enc_frozen.T, enc_adapter, text_rows,
+        norm_gain.reshape(-1, 128), value_weight, value_bias.reshape(-1, 128), llm_frozen.T, llm_adapter,
+        targets, dest_owner.T, seq_length.reshape(1, 1),
     )
     return grad_enc, grad_llm.reshape(RG, KV)
 

time: 105 us -> 87 us (0.83)
  local copies, waits for them, and re-layouts: 12.8 us -> 3.24 us
  Pallas kernels: 90.4 us -> 82.3 us
    pallas_call x1, Pallas kernels: 90.4 us -> 82.3 us  [body(): pl.pallas_call(functools.partial(kernel, sizes), out_shape=(jax.ShapeDtyp...]
    unnamed x5 -> x2, local copies, waits for them, and re-layouts: 8.9 us -> 3.24 us
    reshape x3 -> x0, local copies, waits for them, and re-layouts: 3.92 us -> none  [the longest x1 1.35 us: body(): norm_gain.reshape(1, D)]
where the time goes in v2:
time: 87 us; the launch traced here: 86.8 us
  Pallas kernels  82.3 us (95%)
  local copies, waits for them, and re-layouts  3.24 us (4%)
  between operations  1.29 us (1%)
    pallas_call x1, Pallas kernels, body(): pl.pallas_call(functools.partial(kernel, sizes), out_shape=(jax.ShapeDtyp...  82.3 us
    unnamed x2, local copies, waits for them, and re-layouts  3.24 us

profile of v2, /device:TPU:0, one launch (start us, length us, event | category | flops | bytes accessed | tf_op | source)
XLA Modules:
  0.0 86.8 jit_solution(13417312964391207754)
XLA Ops:
  1.3 82.3 %shard_map.149 = (f32[32,2048]{1,0:T(8,128)}, f32[2,16,1024]{2,1,0:T(8,128)}) custom-call(bf16[64,5120]{1,0:T(8,128)(2,1)} %hidden.1, bf16[5120,2048]{1,0:T(8,128)(2,1)} %enc_weight.1, bf16[16,128]{1,0:T(8,128)(2,1)} %bitcast.13, bf16[64,5120]{1,0:T(8,128)(2,1)} %bitcast.9, bf16[64,2048]{1,0:T(8,128)(2,1)} %enc_adapter.1, bf16[160,8192]{1,0:T(8,128)(2,1)} %text_rows.1, ...), custom_call_target="tpu_custom_call" | custom-call | tf_op jit(solution)/shard_map/pallas_call | solution.py:606
  83.5 1.7 %copy.19 = f32[32,2048]{1,0:T(8,128)} copy(f32[32,2048]{1,0:T(8,128)} %get-tuple-element.8) | data formatting | bytes 524288
  85.2 1.6 %copy.20 = f32[32,1024]{1,0:T(8,128)} copy(f32[32,1024]{1,0:T(8,128)} %bitcast.10) | data formatting | bytes 262144

commit v3 on v2

--- a/solution.py
+++ b/solution.py
@@ -8,6 +8,9 @@
 from jax.sharding import PartitionSpec as P
 
 epsilon = 1e-06
+TG_AT = 0
+W_AT = 1
+NORM_AT = 1
 F32 = jnp.float32
 BF16 = jnp.bfloat16
 MESH = pl.DeviceIdType.MESH
@@ -162,39 +165,46 @@
         cols = pl.ds(k * KC, KC)
         for i in range(1, MP):
             send(hidden.at[pl.ds(c * NH, NH), cols], hid.at[hid_rows, cols], h_ss.at[k, i], h_rs.at[k, i], mp=(m + i) % MP)
-    send_weights()
-    for i in range(1, OWN):
-        other = (owner + i) % OWN
-        od, om = other // MP, other % MP
-        send(tgs.at[od, om], tgr.at[e, m], tg_ss.at[i], tg_rs.at[i], dp=od, mp=om)
     tgr[e, m] = tgs[e, m]
 
-    text_load.wait()
-    TR = 16
-    CW = min(D, 1024)
-
-    def text_norm(i, carry):
-        r = pl.ds(i * TR, TR)
-        total = jnp.zeros((TR, 128), F32)
-        for k in range(D // CW):
-            part = txt[r, pl.ds(k * CW, CW)].astype(F32)
-            part = part * part
-            for n in range(CW // 128):
-                total = total + part[:, n * 128 : (n + 1) * 128]
-        inverse = lax.rsqrt(jnp.sum(total, axis=1, keepdims=True) / D + epsilon)
-        for k in range(D // CW):
-            cols = pl.ds(k * CW, CW)
-            txt[r, cols] = (txt[r, cols].astype(F32) * inverse * gain_ref[:, cols]).astype(BF16)
-        return carry
-
-    lax.fori_loop(0, LR // TR, text_norm, 0)
+    def norm_text():
+        text_load.wait()
+        TR = 16
+        CW = min(D, 1024)
+
+        def text_norm(i, carry):
+            r = pl.ds(i * TR, TR)
+            total = jnp.zeros((TR, 128), F32)
+            for k in range(D // CW):
+                part = txt[r, pl.ds(k * CW, CW)].astype(F32)
+                part = part * part
+                for n in range(CW // 128):
+                    total = total + part[:, n * 128 : (n + 1) * 128]
+            inverse = lax.rsqrt(jnp.sum(total, axis=1, keepdims=True) / D + epsilon)
+            for k in range(D // CW):
+                cols = pl.ds(k * CW, CW)
+                txt[r, cols] = (txt[r, cols].astype(F32) * inverse * gain_ref[:, cols]).astype(BF16)
+            return carry
+
+        lax.fori_loop(0, LR // TR, text_norm, 0)
+
+    if NORM_AT == 0:
+        norm_text()
 
     for i in range(1, DP):
         there = at.at[(e + DP - i) % DP, m, pl.ds(low_half, RH), :]
         landed(there, a1_ss.at[i], a1_rs.at[i])
+    if W_AT == 0:
+        send_weights()
     for i in range(1, MP):
         mine = at.at[:, m, pl.ds(low_half, RH), :]
         send(mine, mine, a2_ss.at[i], a2_rs.at[i], mp=(m + i) % MP)
+
+    if W_AT == 1:
+        send_weights()
+
+    if NORM_AT == 1:
+        norm_text()
 
     own_load.wait()
     TN = min(HC, 256)
@@ -242,6 +252,11 @@
         xq[n * TN // Q, :, n * TN % Q : n * TN % Q + TN] = scaled
     pair = e + 1 - 2 * p
     send(xq.at[1 - t0], xr, x_ss, x_rs, dp=pair)
+    if TG_AT == 0:
+        for i in range(1, OWN):
+            other = (owner + i) % OWN
+            od, om = other // MP, other % MP
+            send(tgs.at[od, om], tgr.at[e, m], tg_ss.at[i], tg_rs.at[i], dp=od, mp=om)
 
     for i in range(1, MP):
         there = at.at[:, (m + MP - i) % MP, pl.ds(low_half, RH), :]
@@ -264,6 +279,11 @@
     lor[m] = los[...] + lop[...]
     for i in range(1, MP):
         send(lor.at[m], lor.at[m], lo_ss.at[i], lo_rs.at[i], mp=(m + i) % MP)
+    if TG_AT == 1:
+        for i in range(1, OWN):
+            other = (owner + i) % OWN
+            od, om = other // MP, other % MP
+            send(tgs.at[od, om], tgr.at[e, m], tg_ss.at[i], tg_rs.at[i], dp=od, mp=om)
 
     def text_low(q, carry):
         part = txt[:, pl.ds(pl.multiple_of(q * R, 128), R)]
@@ -299,6 +319,12 @@
     rest = (text_y - high.astype(F32)).astype(BF16)
     text_grad = (dot(text_low_m, high) + dot(text_low_m, rest)) * scale
 
+    if TG_AT == 2:
+        for i in range(1, OWN):
+            other = (owner + i) % OWN
+            od, om = other // MP, other % MP
+            send(tgs.at[od, om], tgr.at[e, m], tg_ss.at[i], tg_rs.at[i], dp=od, mp=om)
+
     for i in range(QB):
         landed(wq.at[i], w_ss.at[0], w_rs.at[i])
 
@@ -320,7 +346,7 @@
     landed(vpr.at[p], vp_ss.at[0], vp_rs.at[0])
     landed(vpr.at[1 - p], vp_ss.at[1], vp_rs.at[1])
     for i in range(2):
-        both = (vown[i] + vpr[i].astype(F32)).astype(BF16)
+        both = (vown[i] + vpr[i]).astype(BF16)
         for j in range(MP):
             vs[i, j] = both[:, j * NB : (j + 1) * NB]
     for i in range(1, 2 * MP):
@@ -588,7 +614,7 @@
         V((2, BT, Q), BF16), V((BT, Q), BF16), V((QB, R, KV), BF16), V((DP, MP, RANK, R), BF16), V((LR, D), BF16),
         V((MP, 2, RANK, Q), BF16), V((2, MP, RANK, Q), BF16), V((DP, MP, ST, NB), BF16), V((DP, MP, ST, NB), BF16),
         V((RL, BT), F32), V((MP, RL, BT), F32),
-        V((2, BT, KH), F32), V((2, BT, KH), BF16), V((2, BT, KH), BF16),
+        V((2, BT, KH), F32), V((2, BT, KH), F32), V((2, BT, KH), F32),
         V((2, MP, BT, NB), BF16), V((2, MP, BT, NB), BF16),
         V((RL, BT), F32),
         V((RANK, KH), F32), V((RANK, KH), F32), V((DP, MP, RD, NB), F32), V((DP, MP, RD, NB), F32),

time: 87 us -> 86.4 us (level)
  no operation moved by 1% of the time
where the time goes in v3:
time: 86.4 us; the launch traced here: 86.1 us
  Pallas kernels  81.6 us (94%)
  local copies, waits for them, and re-layouts  3.24 us (4%)
  between operations  1.29 us (1%)
    pallas_call x1, Pallas kernels, body(): pl.pallas_call(functools.partial(kernel, sizes), out_shape=(jax.ShapeDtyp...  81.6 us
    unnamed x2, local copies, waits for them, and re-layouts  3.24 us

profile of v3, /device:TPU:0, one launch (start us, length us, event | category | flops | bytes accessed | tf_op | source)
XLA Modules:
  0.0 86.1 jit_solution(15702604507577786832)
XLA Ops:
  1.3 81.6 %shard_map.149 = (f32[32,2048]{1,0:T(8,128)}, f32[2,16,1024]{2,1,0:T(8,128)}) custom-call(bf16[64,5120]{1,0:T(8,128)(2,1)} %hidden.1, bf16[5120,2048]{1,0:T(8,128)(2,1)} %enc_weight.1, bf16[16,128]{1,0:T(8,128)(2,1)} %bitcast.13, bf16[64,5120]{1,0:T(8,128)(2,1)} %bitcast.9, bf16[64,2048]{1,0:T(8,128)(2,1)} %enc_adapter.1, bf16[160,8192]{1,0:T(8,128)(2,1)} %text_rows.1, ...), custom_call_target="tpu_custom_call" | custom-call | tf_op jit(solution)/shard_map/pallas_call | solution.py:632
  82.8 1.7 %copy.19 = f32[32,2048]{1,0:T(8,128)} copy(f32[32,2048]{1,0:T(8,128)} %get-tuple-element.8) | data formatting | bytes 524288
  84.5 1.6 %copy.20 = f32[32,1024]{1,0:T(8,128)} copy(f32[32,1024]{1,0:T(8,128)} %bitcast.10) | data formatting | bytes 262144

commit v4 on v3

--- a/solution.py
+++ b/solution.py
@@ -520,7 +520,7 @@
         landed(s2r.at[(e + DP - i) % DP], s2_ss.at[i], s2_rs.at[i])
     for i in range(DP):
         result = result - s2r[i].astype(F32)
-    fo[...] = result.astype(BF16)
+    fo[...] = result
     UH = UN // 2
     f_core = u // UH
     f_unit = u % UH
@@ -620,7 +620,7 @@
         V((RANK, KH), F32), V((RANK, KH), F32), V((DP, MP, RD, NB), F32), V((DP, MP, RD, NB), F32),
         V((8, BT), F32), V((2 * MP, 8, BT), F32), V((DP, 2, RD, NB), F32), V((DP, 2, RD, NB), F32),
         V((RD, NB), F32), V((2, 2, MP, RD, NB), F32), V((RD, NB), F32),
-        V((2, UN, RU, Q), BF16), V((DP, RU, Q), BF16), V((RU, Q), BF16), V((UN // 2, 2, 2, RU, Q), BF16),
+        V((2, UN, RU, Q), BF16), V((DP, RU, Q), BF16), V((RU, Q), F32), V((UN // 2, 2, 2, RU, Q), F32),
         S((NK,)), S(()), S(()), S((NK, MP)), S((NK, MP)), S((NK, MP)), S((NK, MP)),
         S(((UN + 1) // 2,)), S((QB,)), S(()), S(()), S((DP,)), S((DP,)), S((MP,)), S((MP,)),
         S(()), S(()), S((OWN,)), S((OWN,)), S(()), S(()), S((2 * MP,)), S((2 * MP,)), S((2 * MP,)), S((2 * MP,)),

time: 86.4 us -> 88.5 us (1.024)
  Pallas kernels: 81.6 us -> 83 us
    pallas_call x1, Pallas kernels: 81.6 us -> 83 us  [body(): pl.pallas_call(functools.partial(kernel, sizes), out_shape=(jax.ShapeDtyp...]
where the time goes in v4:
time: 88.5 us; the launch traced here: 87.5 us
  Pallas kernels  83 us (94%)
  local copies, waits for them, and re-layouts  3.24 us (4%)
  between operations  1.29 us (1%)
    pallas_call x1, Pallas kernels, body(): pl.pallas_call(functools.partial(kernel, sizes), out_shape=(jax.ShapeDtyp...  83 us
    unnamed x2, local copies, waits for them, and re-layouts  3.24 us

profile of v4, /device:TPU:0, one launch (start us, length us, event | category | flops | bytes accessed | tf_op | source)
XLA Modules:
  0.0 87.5 jit_solution(9226219521681858627)
XLA Ops:
  1.3 83.0 %shard_map.149 = (f32[32,2048]{1,0:T(8,128)}, f32[2,16,1024]{2,1,0:T(8,128)}) custom-call(bf16[64,5120]{1,0:T(8,128)(2,1)} %hidden.1, bf16[5120,2048]{1,0:T(8,128)(2,1)} %enc_weight.1, bf16[16,128]{1,0:T(8,128)(2,1)} %bitcast.13, bf16[64,5120]{1,0:T(8,128)(2,1)} %bitcast.9, bf16[64,2048]{1,0:T(8,128)(2,1)} %enc_adapter.1, bf16[160,8192]{1,0:T(8,128)(2,1)} %text_rows.1, ...), custom_call_target="tpu_custom_call" | custom-call | tf_op jit(solution)/shard_map/pallas_call | solution.py:632
  84.3 1.7 %copy.19 = f32[32,2048]{1,0:T(8,128)} copy(f32[32,2048]{1,0:T(8,128)} %get-tuple-element.8) | data formatting | bytes 524288
  86.0 1.6 %copy.20 = f32[32,1024]{1,0:T(8,128)} copy(f32[32,1024]{1,0:T(8,128)} %bitcast.10) | data formatting | bytes 262144
